TPU v7x, 256 devices: a 4x2x16 block of a 4x16x16 slice. The times are simulated.
256 devices in a mesh: groups: 2 (over y), px: 64 (over z, x), py: 2 (over core).
Axes of the slice: x: 4, y: 2, z: 16, core: 2. Of those that a mesh axis runs over, the one named last changes fastest.
The devices are a block of a 4x16x16 slice.
Arguments:
- field: bfloat16 [2, 20, 384, 192, 128], P('groups', None, 'px', 'py'), parts along dimension 0, may hold values from -6 to 6
- spectral_weight: bfloat16 [2, 20, 20, 1536, 96], P(None, None, None, ('py', 'px')), may hold values from -6 to 6
- pointwise_weight: bfloat16 [20, 20], replicated, may hold values from -1.25 to 1.25
- bias: float32 [20], replicated, may hold values from -3 to 3
Outputs:
- mixed_field: bfloat16 [2, 20, 384, 192, 128], P('groups', None, 'px', 'py'), parts along dimension 0
There are 2 independent parts, one for each index of `groups`. A program takes and returns all parts, laid end to end along the dimension named above; an argument that names none is the same for every part. Nothing has to cross between parts.
All inputs are finite; a program needn't handle non-finite values.
Results may differ from a plain program's by a relative error of at most 0.001.
Values sent between devices are 32-bit elements; how exact they have to be, the bound alone decides.
No kernel may reach another device: no remote copies, remote signals or barrier semaphores. Data moves between devices by JAX's collectives and lax.ppermute only.
A program may use at most 128 MiB of HBM per device.

v0:
```python
import functools
import math

import jax
import jax.numpy as jnp
import numpy as np
from jax import lax
from jax.experimental import pallas as pl
from jax.experimental.pallas import tpu as pltpu
from jax.sharding import PartitionSpec as P

NX = 384
NY = 192
NZ = 128
MX = 96
MY = 48
MZ = 32

LANES = 128
QUAD = 4
Y_BLOCKS = 4
M = MY // Y_BLOCKS
MP = 16
HALF = 64
VMEM_LIMIT = 60 * 1024 * 1024


def kept(length, retained):
    index = np.arange(retained)
    return np.where(index < retained // 2, index, length - retained + index)


def angles(frequency, positions, length):
    return 2 * np.pi * ((frequency[:, None] * positions[None, :]) % length) / length


def halves(table):
    high = table.astype(np.float32).astype(jnp.bfloat16)
    low = (table - high.astype(np.float64)).astype(np.float32).astype(jnp.bfloat16)
    return np.stack([high, low])


def split(value):
    high = value.astype(jnp.bfloat16)
    low = (value - high.astype(jnp.float32)).astype(jnp.bfloat16)
    return high, low


def dot(a, b, contract=((1,), (0,))):
    return lax.dot_general(a, b, (contract, ((), ())), preferred_element_type=jnp.float32)


def z_order(y_devices):
    order = np.arange(MZ).reshape(y_devices, MZ // y_devices)
    return [np.concatenate([order[d], np.delete(order, d, 0).reshape(-1)]) for d in range(y_devices)]


def z_forward_table(y_devices):
    tables = []
    for kz in z_order(y_devices):
        angle = angles(kz, np.arange(NZ), NZ).T
        table = np.zeros((QUAD, NZ, 2, QUAD, MZ))
        for c in range(QUAD):
            table[c, :, 0, c] = np.cos(angle)
            table[c, :, 1, c] = -np.sin(angle)
        tables.append(halves(table.reshape(QUAD * NZ, 2 * QUAD * MZ)))
    return np.stack(tables)


def y_forward_table(y_devices):
    tables = []
    rows = NY // y_devices
    for d in range(y_devices):
        angle = angles(kept(NY, MY), d * rows + np.arange(rows), NY)
        table = np.zeros((2, Y_BLOCKS, MP, rows))
        table[0, :, :M] = np.cos(angle).reshape(Y_BLOCKS, M, rows)
        table[1, :, :M] = np.sin(angle).reshape(Y_BLOCKS, M, rows)
        tables.append(halves(table.reshape(2 * Y_BLOCKS * MP, rows)))
    return np.stack(tables)


def x_table():
    angle = angles(kept(NX, MX), np.arange(NX), NX).T
    table = np.zeros((NX, 2, LANES))
    table[:, 0, :MX] = np.cos(angle)
    table[:, 1, :MX] = np.sin(angle)
    return halves(table.reshape(NX, 2 * LANES))


def y_inverse_table(y_devices):
    tables = []
    rows = NY // y_devices
    for d in range(y_devices):
        angle = angles(kept(NY, MY), d * rows + np.arange(rows), NY).T
        table = np.zeros((2, rows, 2, Y_BLOCKS, MP))
        cosine = np.cos(angle).reshape(rows, Y_BLOCKS, M)
        sine = np.sin(angle).reshape(rows, Y_BLOCKS, M)
        table[0, :, 0, :, :M] = cosine
        table[0, :, 1, :, :M] = -sine
        table[1, :, 0, :, :M] = sine
        table[1, :, 1, :, :M] = cosine
        tables.append(halves(table.reshape(2 * rows, 2 * Y_BLOCKS * MP)))
    return np.stack(tables)


def z_inverse_table(y_devices):
    tables = []
    for kz in z_order(y_devices):
        angle = angles(kz, np.arange(NZ), NZ)
        weight = np.where(kz == 0, 1.0, 2.0)[:, None] / (NX * NY * NZ)
        table = np.zeros((2, QUAD, MZ, QUAD, NZ))
        for c in range(QUAD):
            table[0, c, :, c] = np.cos(angle) * weight
            table[1, c, :, c] = -np.sin(angle) * weight
        tables.append(halves(table.reshape(2 * QUAD * MZ, QUAD * NZ)))
    return np.stack(tables)


def forward_kernel(place, field, z_table, y_table, own, other, rows):
    x = pl.program_id(0)
    channels = field.shape[0]
    groups = channels // QUAD
    per_x = QUAD * MZ
    half = MZ // 2
    stride = Y_BLOCKS * own.shape[1]
    for g in range(groups):
        cells = jnp.concatenate([field[QUAD * g + c, 0] for c in range(QUAD)], 1)
        z_hat = dot(cells, z_table[0, 0]) + dot(cells, z_table[0, 1])
        high, low = split(z_hat)
        parts = dot(y_table[0, 0], high) + dot(y_table[0, 0], low) + dot(y_table[0, 1], high)
        size = Y_BLOCKS * MP
        real = parts[:size, :per_x] + parts[size:, per_x:]
        imag = parts[:size, per_x:] - parts[size:, :per_x]
        for block in range(Y_BLOCKS):
            for s, value in enumerate((real, imag)):
                rows[block, pl.ds(s * HALF + g * M, MP), :] = value[block * MP : (block + 1) * MP]
    del place
    own_rows = own.reshape(own.shape[0] * own.shape[1], LANES)
    other_rows = other.reshape(other.shape[0] * other.shape[1], LANES)
    for block in range(Y_BLOCKS):
        turned = rows[block, :LANES, :].T
        for c in range(QUAD):
            start = block * own.shape[1] + x * QUAD + c
            at = pl.ds(start, half, stride=stride)
            own_rows[at, :] = turned[c * MZ : c * MZ + half]
            other_rows[at, :] = turned[c * MZ + half : (c + 1) * MZ]


def forward(place, field, y_devices, x_devices):
    channels, x_local, y_local, _ = field.shape
    z_table, y_table = z_forward_table(y_devices), y_forward_table(y_devices)
    payload = jax.ShapeDtypeStruct((x_devices, x_local * QUAD, LANES), jnp.float32)
    whole = pl.BlockSpec(payload.shape, lambda x, p: (0, 0, 0))
    return pl.pallas_call(
        forward_kernel,
        out_shape=(payload, payload),
        grid_spec=pltpu.PrefetchScalarGridSpec(
            num_scalar_prefetch=1,
            grid=(x_local,),
            in_specs=[
                pl.BlockSpec((channels, 1, y_local, NZ), lambda x, p: (0, x, 0, 0)),
                pl.BlockSpec((1, *z_table.shape[1:]), lambda x, p: (p[0], 0, 0, 0)),
                pl.BlockSpec((1, *y_table.shape[1:]), lambda x, p: (p[0], 0, 0, 0)),
            ],
            out_specs=[whole, whole],
            scratch_shapes=[pltpu.VMEM((Y_BLOCKS, LANES + MP, LANES), jnp.float32)],
        ),
        compiler_params=pltpu.CompilerParams(
            dimension_semantics=("arbitrary",), vmem_limit_bytes=VMEM_LIMIT
        ),
        name="forward",
    )(place, field, jnp.asarray(z_table), jnp.asarray(y_table))


def mix_kernel(payload, weights, table, result, spectrum, mixed):
    channels = weights.shape[1]
    groups = channels // QUAD
    source = payload.reshape(payload.shape[0] * payload.shape[1], LANES)
    target = result.reshape(result.shape[0] * result.shape[1], LANES)
    for c in range(QUAD):
        high, low = split(source[pl.ds(c, NX, stride=QUAD), :])
        over_x = ((0,), (0,))
        parts = dot(high, table[0], over_x) + dot(low, table[0], over_x) + dot(high, table[1], over_x)
        spectrum[c, 0] = parts[:HALF, :LANES] + parts[HALF:, LANES:]
        spectrum[c, 1] = parts[HALF:, :LANES] - parts[:HALF, LANES:]
    outs = channels // 2
    for first in range(0, channels, outs):
        real = [jnp.zeros((MP, LANES), jnp.float32)] * outs
        imag = [jnp.zeros((MP, LANES), jnp.float32)] * outs
        for i in range(channels):
            g, c = i // QUAD, i % QUAD
            real_in = spectrum[c, 0, pl.ds(g * M, MP), :]
            imag_in = spectrum[c, 1, pl.ds(g * M, MP), :]
            for k in range(outs):
                w_real = weights[0, i, first + k].astype(jnp.float32)
                w_imag = weights[1, i, first + k].astype(jnp.float32)
                real[k] = real[k] + (w_real * real_in - w_imag * imag_in)
                imag[k] = imag[k] + (w_real * imag_in + w_imag * real_in)
        for k in range(outs):
            g, c = (first + k) // QUAD, (first + k) % QUAD
            upper = pl.ds(g * M, MP)
            lower = pl.ds(HALF + g * M, MP)
            mixed[c, upper, :LANES] = real[k]
            mixed[c, upper, LANES:] = -imag[k]
            mixed[c, lower, :LANES] = imag[k]
            mixed[c, lower, LANES:] = real[k]
    del groups
    for c in range(QUAD):
        high, low = split(mixed[c, :LANES, :])
        over_k = ((1,), (1,))
        back = dot(table[0], high, over_k) + dot(table[0], low, over_k) + dot(table[1], high, over_k)
        target[pl.ds(c, NX, stride=QUAD), :] = back


def mix(payload, weights):
    table = x_table()
    vmem = pl.BlockSpec(memory_space=pltpu.VMEM)
    return pl.pallas_call(
        mix_kernel,
        out_shape=jax.ShapeDtypeStruct(payload.shape, jnp.float32),
        in_specs=[vmem, vmem, vmem],
        out_specs=vmem,
        scratch_shapes=[
            pltpu.VMEM((QUAD, 2, HALF, LANES), jnp.float32),
            pltpu.VMEM((QUAD, LANES + MP, 2 * LANES), jnp.float32),
        ],
        compiler_params=pltpu.CompilerParams(vmem_limit_bytes=VMEM_LIMIT),
        name="mix",
    )(payload, weights, jnp.asarray(table))


def inverse_kernel(place, own, other, field, y_table, z_table, local, bias, out, rows, modes, total):
    del place
    x = pl.program_id(0)
    channels, _, y_local, _ = field.shape
    groups = channels // QUAD
    half = MZ // 2
    stride = Y_BLOCKS * own.shape[1]
    own_rows = own.reshape(own.shape[0] * own.shape[1], LANES)
    other_rows = other.reshape(other.shape[0] * other.shape[1], LANES)
    for block in range(Y_BLOCKS):
        for c in range(QUAD):
            start = block * own.shape[1] + x * QUAD + c
            at = pl.ds(start, half, stride=stride)
            rows[c * MZ : c * MZ + half] = own_rows[at, :]
            rows[c * MZ + half : (c + 1) * MZ] = other_rows[at, :]
        modes[block] = rows[...].T
    for g in range(groups):
        inputs = jnp.concatenate(
            [modes[block, pl.ds(s * HALF + g * M, MP), :] for s in range(2) for block in range(Y_BLOCKS)], 0
        )
        high, low = split(inputs)
        lines = dot(y_table[0, 0], high) + dot(y_table[0, 0], low) + dot(y_table[0, 1], high)
        lines = jnp.concatenate([lines[:y_local], lines[y_local:]], 1)
        high, low = split(lines)
        cells = dot(high, z_table[0, 0]) + dot(low, z_table[0, 0]) + dot(high, z_table[0, 1])
        for c in range(QUAD):
            total[QUAD * g + c] = cells[:, c * NZ : (c + 1) * NZ]
    step = MP
    for y in range(0, y_local, 2 * step):
        pair = [
            field[:, 0, y + j * step : y + (j + 1) * step, :].reshape(channels * step, NZ) for j in range(2)
        ]
        mixed = dot(local[...], jnp.concatenate(pair, 1))
        for o in range(channels):
            for j in range(2):
                at = slice(y + j * step, y + (j + 1) * step)
                value = mixed[o * step : (o + 1) * step, j * NZ : (j + 1) * NZ]
                value = value + total[o, at, :] + bias[o]
                inner = math.sqrt(2 / math.pi) * (value + 0.044715 * (value * value * value))
                out[o, 0, at, :] = (0.5 * value * (1.0 + jnp.tanh(inner))).astype(out.dtype)


def inverse(place, own, other, field, local, bias, y_devices):
    channels, x_local, y_local, _ = field.shape
    z_table, y_table = z_inverse_table(y_devices), y_inverse_table(y_devices)
    whole = pl.BlockSpec(own.shape, lambda x, p: (0, 0, 0))
    cells = pl.BlockSpec((channels, 1, y_local, NZ), lambda x, p: (0, x, 0, 0))
    return pl.pallas_call(
        inverse_kernel,
        out_shape=jax.ShapeDtypeStruct(field.shape, field.dtype),
        grid_spec=pltpu.PrefetchScalarGridSpec(
            num_scalar_prefetch=1,
            grid=(x_local,),
            in_specs=[
                whole,
                whole,
                cells,
                pl.BlockSpec((1, *y_table.shape[1:]), lambda x, p: (p[0], 0, 0, 0)),
                pl.BlockSpec((1, *z_table.shape[1:]), lambda x, p: (p[0], 0, 0, 0)),
                pl.BlockSpec(local.shape, lambda x, p: (0, 0)),
                pl.BlockSpec(memory_space=pltpu.SMEM),
            ],
            out_specs=cells,
            scratch_shapes=[
                pltpu.VMEM((LANES, LANES), jnp.float32),
                pltpu.VMEM((Y_BLOCKS, LANES, LANES), jnp.float32),
                pltpu.VMEM((channels, y_local, NZ), jnp.float32),
            ],
        ),
        compiler_params=pltpu.CompilerParams(
            dimension_semantics=("arbitrary",), vmem_limit_bytes=VMEM_LIMIT
        ),
        name="inverse",
    )(place, own, other, field, jnp.asarray(y_table), jnp.asarray(z_table), local, bias)


def spread_weights(spectral_weight):
    m, k = spectral_weight.shape[3:]
    return jnp.pad(spectral_weight, ((0, 0), (0, 0), (0, 0), (0, MP - m), (0, LANES - k)))


def local_matrix(pointwise_weight):
    channels = pointwise_weight.shape[0]
    eye = jnp.eye(MP, dtype=pointwise_weight.dtype)
    matrix = pointwise_weight.T[:, None, :, None] * eye[None, :, None, :]
    return matrix.reshape(channels * MP, channels * MP)


def swapped(x, axis):
    devices = lax.axis_size(axis)
    return lax.ppermute(x, axis, [(d, (d + 1) % devices) for d in range(devices)])


def per_device(field, spectral_weight, pointwise_weight, bias):
    y_devices, x_devices = lax.axis_size("py"), lax.axis_size("px")
    place = lax.axis_index("py").astype(jnp.int32).reshape(1)
    cells = field[0]
    weights = spread_weights(spectral_weight)
    local = local_matrix(pointwise_weight)
    own, other = forward(place, cells, y_devices, x_devices)
    payload = own + swapped(other, "py")
    received = lax.all_to_all(payload, "px", 0, 0, tiled=True)
    result = mix(received, weights)
    own = lax.all_to_all(result, "px", 0, 0, tiled=True)
    other = swapped(own, "py")
    return inverse(place, own, other, cells, local, bias, y_devices)[None]


def solution(mesh):
    in_specs = (
        P("groups", None, "px", "py", None),
        P(None, None, None, ("py", "px"), None),
        P(),
        P(),
    )
    out_specs = P("groups", None, "px", "py", None)
    return jax.shard_map(per_device, mesh=mesh, in_specs=in_specs, out_specs=out_specs, check_vma=False)
```

profile of v0, /device:TPU:33, one launch (start us, length us, event | category | flops | bytes accessed | tf_op | source)
XLA Modules:
  0.0 164.3 jit_solution(17954324383267449795)
XLA Ops:
  0.0 13.9 %forward.1 = (f32[64,24,128]{2,1,0:T(8,128)}, f32[64,24,128]{2,1,0:T(8,128)}) custom-call(s32[1]{0:T(128)} %bitcast.place, bf16[20,6,96,128]{3,2,1,0:T(8,128)(2,1)} %bitcast.4, bf16[2,2,512,256]{3,2,1,0:T(8,128)(2,1)} %constant.17.clone.z_table, bf16[2,2,128,96]{3,2,1,0:T(8,128)(2,1)} %constant.18.clone.y_table), custom_call_target="tpu_custom_call" | custom-call | tf_op jit(solution)/shard_map/forward/pallas_call | solution.py:154
  13.9 0.0 copy-start.2
  13.9 20.4 %collective-permute-start = (f32[64,24,128]{2,1,0:T(8,128)}, f32[64,24,128]{2,1,0:T(8,128)S(1)}, u32[]{:S(2)}, u32[]{:S(2)}) collective-permute-start(f32[64,24,128]{2,1,0:T(8,128)} %get-tuple-element.8), channel_id=1, source_target_pairs={{0,1},{1,0},{2,3},{3,2},{4,5},{5,4},{6,7},{7,6},{8,9},{9,8},{10,11... | collective-permute-start | bytes 2359304 | tf_op jit(solution)/shard_map/ppermute | solution.py:322
  34.3 2.1 %collective-permute-done = f32[64,24,128]{2,1,0:T(8,128)S(1)} collective-permute-done((f32[64,24,128]{2,1,0:T(8,128)}, f32[64,24,128]{2,1,0:T(8,128)S(1)}, u32[]{:S(2)}, u32[]{:S(2)}) %collective-permute-start) | collective-permute-done | bytes 786464 | tf_op jit(solution)/shard_map/ppermute | solution.py:322
  36.4 2.1 %add.5 = f32[64,24,128]{2,1,0:T(8,128)} add(f32[64,24,128]{2,1,0:T(8,128)} %get-tuple-element.7, f32[64,24,128]{2,1,0:T(8,128)S(1)} %collective-permute-done) | non-fusion elementwise | flops 196608 | bytes 2359296 | tf_op jit(solution)/shard_map/add | solution.py:332
  38.5 9.8 %all-to-all-start = ((f32[64,24,128]{2,1,0:T(8,128)}), f32[64,24,128]{2,1,0:T(8,128)S(1)}, u32[]{:S(2)}, u32[]{:S(2)}) async-start(f32[64,24,128]{2,1,0:T(8,128)} %add.5), calls=%async_computation | async-start | bytes 1572864 | tf_op jit(solution)/shard_map/all_to_all | solution.py:333
  48.3 0.0 copy-done.2
  48.3 0.8 copy.12
  49.1 2.7 %pad.4.weights = bf16[2,20,20,16,128]{4,3,2,1,0:T(8,128)(2,1)} pad(bf16[2,20,20,12,96]{4,3,2,1,0:T(8,128)(2,1)S(1)} %copy.12, bf16[]{:T(256)} %constant.16.clone.1), padding=0_0x0_0x0_0x0_4x0_32 | pad | bytes 5120002 | tf_op jit(solution)/shard_map/jit(_pad)/pad | solution.py:310
  51.8 0.0 copy-start.4
  51.8 36.6 %all-to-all-done.payload = f32[64,24,128]{2,1,0:T(8,128)S(1)} async-done(((f32[64,24,128]{2,1,0:T(8,128)}), f32[64,24,128]{2,1,0:T(8,128)S(1)}, u32[]{:S(2)}, u32[]{:S(2)}) %all-to-all-start) | async-done | bytes 786464 | tf_op jit(solution)/shard_map/all_to_all | solution.py:333
  88.3 0.0 copy-start.1
  88.3 0.9 copy-done.1
  89.2 5.6 %mix.1 = f32[64,24,128]{2,1,0:T(8,128)} custom-call(f32[64,24,128]{2,1,0:T(8,128)} %copy-done.1, bf16[2,20,20,16,128]{4,3,2,1,0:T(8,128)(2,1)} %pad.4.weights, bf16[2,384,256]{2,1,0:T(8,128)(2,1)} %constant.19.clone.table), custom_call_target="tpu_custom_call" | custom-call | tf_op jit(solution)/shard_map/mix/pallas_call | solution.py:218
  94.8 47.8 %all_to_all.10.own = f32[64,24,128]{2,1,0:T(8,128)S(1)} all-to-all(f32[64,24,128]{2,1,0:T(8,128)} %mix.1), channel_id=1, replica_groups=mesh['groups'=2,'px'=64,'py'=2] {'px'}, dimensions={0} | all-to-all | bytes 1572864 | tf_op jit(solution)/shard_map/all_to_all | solution.py:335
  142.6 0.0 copy-start
  142.6 5.3 %collective-permute-start.1 = (f32[64,24,128]{2,1,0:T(8,128)S(1)}, f32[64,24,128]{2,1,0:T(8,128)S(1)}, u32[]{:S(2)}, u32[]{:S(2)}) collective-permute-start(f32[64,24,128]{2,1,0:T(8,128)S(1)} %all_to_all.10.own), channel_id=1, source_target_pairs={{0,1},{1,0},{2,3},{3,2},{4,5},{5,4},{6,7},{7,6},{8,9},{9,8},{10,11... | collective-permute-start | bytes 2359304 | tf_op jit(solution)/shard_map/ppermute | solution.py:322
  147.9 0.0 copy-done.4
  147.9 0.1 copy.13
  148.0 0.2 broadcast_multiply_fusion
  148.2 1.8 %mul.20.local = bf16[320,320]{1,0:T(8,128)(2,1)} reshape(bf16[20,16,20,16]{3,2,1,0:T(8,128)(2,1)S(1)} %broadcast_multiply_fusion) | data formatting | bytes 409600 | tf_op jit(solution)/shard_map/mul | solution.py:316
  150.1 0.0 collective-permute-done.1.other
  150.1 0.0 copy-done
  150.1 0.0 copy-start.3
  150.1 0.9 copy-done.3
  151.0 13.3 %inverse.1 = bf16[20,6,96,128]{3,2,1,0:T(8,128)(2,1)} custom-call(s32[1]{0:T(128)} %bitcast.place, f32[64,24,128]{2,1,0:T(8,128)} %copy-done, f32[64,24,128]{2,1,0:T(8,128)} %copy-done.3, bf16[20,6,96,128]{3,2,1,0:T(8,128)(2,1)} %bitcast.5, bf16[2,2,192,128]{3,2,1,0:T(8,128)(2,1)} %constant.20.clone.y_table, ...), custom_call_target="tpu_custom_call" | custom-call | tf_op jit(solution)/shard_map/inverse/pallas_call | solution.py:279
  (1 shorter events, 0.0 us)
Async XLA Ops:
  13.9 34.4 %copy-start.2 = (bf16[2,20,20,12,96]{4,0,3,2,1:T(2,128)(2,1)S(1)}, bf16[2,20,20,12,96]{4,0,3,2,1:T(2,128)(2,1)}, u32[]{:S(2)}) copy-start(bf16[2,20,20,12,96]{4,0,3,2,1:T(2,128)(2,1)} %param.10) | copy-start | bytes 5529604
  13.9 22.5 %collective-permute-start = (f32[64,24,128]{2,1,0:T(8,128)}, f32[64,24,128]{2,1,0:T(8,128)S(1)}, u32[]{:S(2)}, u32[]{:S(2)}) collective-permute-start(f32[64,24,128]{2,1,0:T(8,128)} %get-tuple-element.8), channel_id=1, source_target_pairs={{0,1},{1,0},{2,3},{3,2},{4,5},{5,4},{6,7},{7,6},{8,9},{9,8},{10,11... | collective-permute-start | bytes 2359304 | tf_op jit(solution)/shard_map/ppermute | solution.py:322
  38.5 49.8 %all-to-all-start = ((f32[64,24,128]{2,1,0:T(8,128)}), f32[64,24,128]{2,1,0:T(8,128)S(1)}, u32[]{:S(2)}, u32[]{:S(2)}) async-start(f32[64,24,128]{2,1,0:T(8,128)} %add.5), calls=%async_computation | async-start | bytes 1572864 | tf_op jit(solution)/shard_map/all_to_all | solution.py:333
  51.8 96.1 %copy-start.4 = (bf16[20,20]{1,0:T(8,128)(2,1)S(1)}, bf16[20,20]{1,0:T(8,128)(2,1)}, u32[]{:S(2)}) copy-start(bf16[20,20]{1,0:T(8,128)(2,1)} %param.11) | copy-start | bytes 2404
  88.3 0.9 copy-start.1
  142.6 7.5 %copy-start = (f32[64,24,128]{2,1,0:T(8,128)}, f32[64,24,128]{2,1,0:T(8,128)S(1)}, u32[]{:S(2)}) copy-start(f32[64,24,128]{2,1,0:T(8,128)S(1)} %all_to_all.10.own) | copy-start | bytes 2359300
  142.6 7.5 %collective-permute-start.1 = (f32[64,24,128]{2,1,0:T(8,128)S(1)}, f32[64,24,128]{2,1,0:T(8,128)S(1)}, u32[]{:S(2)}, u32[]{:S(2)}) collective-permute-start(f32[64,24,128]{2,1,0:T(8,128)S(1)} %all_to_all.10.own), channel_id=1, source_target_pairs={{0,1},{1,0},{2,3},{3,2},{4,5},{5,4},{6,7},{7,6},{8,9},{9,8},{10,11... | collective-permute-start | bytes 2359304 | tf_op jit(solution)/shard_map/ppermute | solution.py:322
  150.1 0.9 copy-start.3
where the time goes:
time: 165 us; the launch traced here: 164 us
  blocking collectives  47.8 us (29%)
  waiting for transfers between devices  38.7 us (23%)
  starting transfers between devices  35.5 us (22%)
  Pallas kernels  32.8 us (20%)
  local copies, waits for them, and re-layouts  7.19 us (4%)
  other arithmetic  2.29 us (1%)
    all_to_all x1, blocking collectives, per_device(): own = lax.all_to_all(result, 'px', 0, 0, tiled=True)  47.8 us
    all_to_all x1, waiting for transfers between devices, per_device(): received = lax.all_to_all(payload, 'px', 0, 0, tiled=True)  36.6 us
    ppermute x2, starting transfers between devices, swapped(): lax.ppermute(x, axis, [(d, (d + 1) % devices) for d in range(devices)])  25.7 us
    pallas_call x1, Pallas kernels, forward(): pl.pallas_call(forward_kernel, out_shape=(payload, payload), grid_spec=pl...  13.9 us
    pallas_call x1, Pallas kernels, inverse(): pl.pallas_call(inverse_kernel, out_shape=jax.ShapeDtypeStruct(field.shape...  13.3 us
    all_to_all x1, starting transfers between devices, per_device(): received = lax.all_to_all(payload, 'px', 0, 0, tiled=True)  9.78 us
    pallas_call x1, Pallas kernels, mix(): pl.pallas_call(mix_kernel, out_shape=jax.ShapeDtypeStruct(payload.shape,...  5.57 us
  transfers between devices with their start and end apart: 3, of which 2 were waited for; matrix products, arithmetic and copies ran while one was open for 3% of the time, Pallas kernels for 0%

commit v1 on v0

v1 whole, which is shorter than its diff:
```python
import functools
import math

import jax
import jax.numpy as jnp
import numpy as np
from jax import lax
from jax.experimental import pallas as pl
from jax.experimental.pallas import tpu as pltpu
from jax.sharding import PartitionSpec as P

NX = 384
NY = 192
NZ = 128
MX = 96
MY = 48
MZ = 32

LANES = 128
QUAD = 4
Y_BLOCKS = 4
M = MY // Y_BLOCKS
MP = 16
HALF = 64
X_STEP = 2
MIB = 1024 * 1024


def kept(length, retained):
    index = np.arange(retained)
    return np.where(index < retained // 2, index, length - retained + index)


def angles(frequency, positions, length):
    return 2 * np.pi * ((frequency[:, None] * positions[None, :]) % length) / length


def halves(table):
    high = table.astype(np.float32).astype(jnp.bfloat16)
    low = (table - high.astype(np.float64)).astype(np.float32).astype(jnp.bfloat16)
    return np.stack([high, low])


def split(value):
    high = value.astype(jnp.bfloat16)
    low = (value - high.astype(jnp.float32)).astype(jnp.bfloat16)
    return high, low


def dot(a, b, contract=((1,), (0,))):
    return lax.dot_general(a, b, (contract, ((), ())), preferred_element_type=jnp.float32)


def z_order(y_devices):
    order = np.arange(MZ).reshape(y_devices, MZ // y_devices)
    return [np.concatenate([order[d], np.delete(order, d, 0).reshape(-1)]) for d in range(y_devices)]


def z_forward_table(y_devices):
    tables = []
    for kz in z_order(y_devices):
        angle = np.tile(angles(kz, np.arange(NZ), NZ).T, (1, QUAD))
        tables.append(halves(np.concatenate([np.cos(angle), -np.sin(angle)], 1)))
    return np.stack(tables)


def stacked(table):
    high, low = halves(table)
    return np.concatenate([np.concatenate([high, high], 1), np.concatenate([low, np.zeros_like(low)], 1)], 0)


def y_forward_table(y_devices):
    tables = []
    rows = NY // y_devices
    for d in range(y_devices):
        angle = angles(kept(NY, MY), d * rows + np.arange(rows), NY)
        table = np.zeros((2, Y_BLOCKS, MP, rows))
        table[0, :, :M] = np.cos(angle).reshape(Y_BLOCKS, M, rows)
        table[1, :, :M] = np.sin(angle).reshape(Y_BLOCKS, M, rows)
        tables.append(stacked(table.reshape(2 * Y_BLOCKS * MP, rows)))
    return np.stack(tables)


def x_table():
    angle = angles(kept(NX, MX), np.arange(NX), NX).T
    table = np.zeros((NX, 2, LANES))
    table[:, 0, :MX] = np.cos(angle)
    table[:, 1, :MX] = np.sin(angle)
    return halves(table.reshape(NX, 2 * LANES))


def y_inverse_table(y_devices):
    tables = []
    rows = NY // y_devices
    for d in range(y_devices):
        angle = angles(kept(NY, MY), d * rows + np.arange(rows), NY).T
        table = np.zeros((2, rows, 2, Y_BLOCKS, MP))
        cosine = np.cos(angle).reshape(rows, Y_BLOCKS, M)
        sine = np.sin(angle).reshape(rows, Y_BLOCKS, M)
        table[0, :, 0, :, :M] = cosine
        table[0, :, 1, :, :M] = -sine
        table[1, :, 0, :, :M] = sine
        table[1, :, 1, :, :M] = cosine
        tables.append(stacked(table.reshape(2 * rows, 2 * Y_BLOCKS * MP)))
    return np.stack(tables)


def z_inverse_table(y_devices):
    tables = []
    for kz in z_order(y_devices):
        angle = angles(kz, np.arange(NZ), NZ)
        weight = np.where(kz == 0, 1.0, 2.0)[:, None] / (NX * NY * NZ)
        cosine = np.tile(np.cos(angle) * weight, (QUAD, 1))
        sine = np.tile(np.sin(angle) * weight, (QUAD, 1))
        tables.append(halves(np.concatenate([cosine, -sine], 0)))
    return np.stack(tables)


def own_block(table, c, dim):
    at = lax.broadcasted_iota(jnp.int32, table.shape, dim) // MZ % QUAD
    return jnp.where(at == c, table.astype(jnp.float32), 0.0).astype(jnp.bfloat16)


def forward_kernel(place, field, z_table, y_table, own, other, spread, z_hat, rows):
    del place
    first_x = pl.program_id(0) * X_STEP

    @pl.when(pl.program_id(0) == 0)
    def _():
        for part in range(2):
            for c in range(QUAD):
                spread[part, c * NZ : (c + 1) * NZ, :] = own_block(z_table[0, part], c, 1)

    channels, _, y_local, _ = field.shape
    groups = channels // QUAD
    per_x = QUAD * MZ
    half = MZ // 2
    size = Y_BLOCKS * MP
    stride = Y_BLOCKS * own.shape[1]
    cells = jnp.concatenate(
        [
            jnp.concatenate([field[QUAD * g + c, i] for c in range(QUAD)], 1)
            for i in range(X_STEP)
            for g in range(groups)
        ],
        0,
    )
    z_hat[...] = dot(cells, spread[0]) + dot(cells, spread[1])
    own_rows = own.reshape(own.shape[0] * own.shape[1], LANES)
    other_rows = other.reshape(other.shape[0] * other.shape[1], LANES)
    for i in range(X_STEP):
        for g in range(groups):
            high, low = split(z_hat[pl.ds((i * groups + g) * y_local, y_local), :])
            parts = dot(y_table[0], jnp.concatenate([high, low], 0))
            parts = parts[: 2 * size] + parts[2 * size :]
            real = parts[:size, :per_x] + parts[size:, per_x:]
            imag = parts[:size, per_x:] - parts[size:, :per_x]
            for block in range(Y_BLOCKS):
                for s, value in enumerate((real, imag)):
                    at = pl.ds(s * HALF + g * M, MP)
                    rows[i, block, at, :] = value[block * MP : (block + 1) * MP]
        for block in range(Y_BLOCKS):
            turned = rows[i, block, :LANES, :].T
            for c in range(QUAD):
                start = block * own.shape[1] + (first_x + i) * QUAD + c
                at = pl.ds(start, half, stride=stride)
                own_rows[at, :] = turned[c * MZ : c * MZ + half]
                other_rows[at, :] = turned[c * MZ + half : (c + 1) * MZ]


def forward(place, field, y_devices, x_devices):
    channels, x_local, y_local, _ = field.shape
    z_table, y_table = z_forward_table(y_devices), y_forward_table(y_devices)
    payload = jax.ShapeDtypeStruct((x_devices, x_local * QUAD, LANES), jnp.float32)
    whole = pl.BlockSpec(payload.shape, lambda x, p: (0, 0, 0))
    lines = X_STEP * (channels // QUAD) * y_local
    return pl.pallas_call(
        forward_kernel,
        out_shape=(payload, payload),
        grid_spec=pltpu.PrefetchScalarGridSpec(
            num_scalar_prefetch=1,
            grid=(x_local // X_STEP,),
            in_specs=[
                pl.BlockSpec((channels, X_STEP, y_local, NZ), lambda x, p: (0, x, 0, 0)),
                pl.BlockSpec((1, *z_table.shape[1:]), lambda x, p: (p[0], 0, 0, 0)),
                pl.BlockSpec((1, *y_table.shape[1:]), lambda x, p: (p[0], 0, 0)),
            ],
            out_specs=[whole, whole],
            scratch_shapes=[
                pltpu.VMEM((2, QUAD * NZ, 2 * QUAD * MZ), jnp.bfloat16),
                pltpu.VMEM((lines, 2 * QUAD * MZ), jnp.float32),
                pltpu.VMEM((X_STEP, Y_BLOCKS, LANES + MP, LANES), jnp.float32),
            ],
        ),
        compiler_params=pltpu.CompilerParams(
            dimension_semantics=("arbitrary",), vmem_limit_bytes=20 * MIB
        ),
        name="forward",
    )(place, field, jnp.asarray(z_table), jnp.asarray(y_table))


def mix_kernel(payload, weights, table, result, spectrum, mixed):
    channels = weights.shape[1]
    source = payload.reshape(payload.shape[0] * payload.shape[1], LANES)
    target = result.reshape(result.shape[0] * result.shape[1], LANES)
    rows = jnp.concatenate([source[pl.ds(c, NX, stride=QUAD), :] for c in range(QUAD)], 1)
    high, low = split(rows.T)
    parts = dot(high, table[0]) + dot(low, table[0]) + dot(high, table[1])
    for c in range(QUAD):
        upper = parts[c * LANES : c * LANES + HALF]
        lower = parts[c * LANES + HALF : (c + 1) * LANES]
        spectrum[c, 0] = upper[:, :LANES] + lower[:, LANES:]
        spectrum[c, 1] = lower[:, :LANES] - upper[:, LANES:]
    outs = channels // 2
    for first in range(0, channels, outs):
        real = [jnp.zeros((MP, LANES), jnp.float32)] * outs
        imag = [jnp.zeros((MP, LANES), jnp.float32)] * outs
        for i in range(channels):
            g, c = i // QUAD, i % QUAD
            real_in = spectrum[c, 0, pl.ds(g * M, MP), :]
            imag_in = spectrum[c, 1, pl.ds(g * M, MP), :]
            for k in range(outs):
                w_real = weights[0, i, first + k].astype(jnp.float32)
                w_imag = weights[1, i, first + k].astype(jnp.float32)
                real[k] = real[k] + (w_real * real_in - w_imag * imag_in)
                imag[k] = imag[k] + (w_real * imag_in + w_imag * real_in)
        for k in range(outs):
            g, c = (first + k) // QUAD, (first + k) % QUAD
            upper = pl.ds(g * M, MP)
            lower = pl.ds(HALF + g * M, MP)
            mixed[c, upper, :LANES] = real[k]
            mixed[c, upper, LANES:] = -imag[k]
            mixed[c, lower, :LANES] = imag[k]
            mixed[c, lower, LANES:] = real[k]
    for c in range(0, QUAD, 2):
        high, low = split(jnp.concatenate([mixed[c, :LANES, :], mixed[c + 1, :LANES, :]], 0))
        over_k = ((1,), (1,))
        back = dot(table[0], high, over_k) + dot(table[0], low, over_k) + dot(table[1], high, over_k)
        target[pl.ds(c, NX, stride=QUAD), :] = back[:, :LANES]
        target[pl.ds(c + 1, NX, stride=QUAD), :] = back[:, LANES:]


def mix(payload, weights):
    table = x_table()
    vmem = pl.BlockSpec(memory_space=pltpu.VMEM)
    return pl.pallas_call(
        mix_kernel,
        out_shape=jax.ShapeDtypeStruct(payload.shape, jnp.float32),
        in_specs=[vmem, vmem, vmem],
        out_specs=vmem,
        scratch_shapes=[
            pltpu.VMEM((QUAD, 2, HALF, LANES), jnp.float32),
            pltpu.VMEM((QUAD, LANES + MP, 2 * LANES), jnp.float32),
        ],
        compiler_params=pltpu.CompilerParams(vmem_limit_bytes=20 * MIB),
        name="mix",
    )(payload, weights, jnp.asarray(table))


def pointwise_kernel(field, local, bias, out):
    channels, steps, y_local, _ = field.shape
    for i in range(steps):
        for y in range(0, y_local, 2 * MP):
            pair = [
                field[:, i, y + j * MP : y + (j + 1) * MP, :].reshape(channels * MP, NZ) for j in range(2)
            ]
            mixed = dot(local[...], jnp.concatenate(pair, 1))
            for o in range(channels):
                for j in range(2):
                    value = mixed[o * MP : (o + 1) * MP, j * NZ : (j + 1) * NZ]
                    out[o, i, y + j * MP : y + (j + 1) * MP, :] = value + bias[o]


def pointwise(field, local, bias):
    channels, x_local, y_local, _ = field.shape
    cells = pl.BlockSpec((channels, 1, y_local, NZ), lambda x: (0, x, 0, 0))
    return pl.pallas_call(
        pointwise_kernel,
        out_shape=jax.ShapeDtypeStruct(field.shape, jnp.float32),
        grid=(x_local,),
        in_specs=[cells, pl.BlockSpec(local.shape, lambda x: (0, 0)), pl.BlockSpec(memory_space=pltpu.SMEM)],
        out_specs=cells,
        compiler_params=pltpu.CompilerParams(
            dimension_semantics=("arbitrary",), vmem_limit_bytes=12 * MIB
        ),
        cost_estimate=pl.CostEstimate(
            flops=2 * field.size * channels * MP, transcendentals=0, bytes_accessed=6 * field.size
        ),
        name="pointwise",
    )(field, local, bias)


def inverse_kernel(place, own, other, base, y_table, z_table, out, spread, rows, modes, lines, total):
    del place
    first_x = pl.program_id(0) * X_STEP

    @pl.when(pl.program_id(0) == 0)
    def _():
        for part in range(2):
            for c in range(QUAD):
                spread[part, :, c * NZ : (c + 1) * NZ] = own_block(z_table[0, part], c, 0)

    channels, _, y_local, _ = base.shape
    groups = channels // QUAD
    half = MZ // 2
    stride = Y_BLOCKS * own.shape[1]
    own_rows = own.reshape(own.shape[0] * own.shape[1], LANES)
    other_rows = other.reshape(other.shape[0] * other.shape[1], LANES)
    for i in range(X_STEP):
        for block in range(Y_BLOCKS):
            for c in range(QUAD):
                start = block * own.shape[1] + (first_x + i) * QUAD + c
                at = pl.ds(start, half, stride=stride)
                rows[i, block, c * MZ : c * MZ + half] = own_rows[at, :]
                rows[i, block, c * MZ + half : (c + 1) * MZ] = other_rows[at, :]
            modes[i, block] = rows[i, block].T
    for g in range(groups):
        inputs = jnp.concatenate(
            [
                jnp.concatenate([modes[i, block, pl.ds(s * HALF + g * M, MP), :] for i in range(X_STEP)], 1)
                for s in range(2)
                for block in range(Y_BLOCKS)
            ],
            0,
        )
        high, low = split(inputs)
        parts = dot(y_table[0], jnp.concatenate([high, low], 0))
        parts = parts[: 2 * y_local] + parts[2 * y_local :]
        for i in range(X_STEP):
            at = pl.ds((i * groups + g) * y_local, y_local)
            for s in range(2):
                high, low = split(parts[s * y_local : (s + 1) * y_local, i * LANES : (i + 1) * LANES])
                lines[0, at, s * LANES : (s + 1) * LANES] = high
                lines[1, at, s * LANES : (s + 1) * LANES] = low
    total[...] = dot(lines[0], spread[0]) + dot(lines[1], spread[0]) + dot(lines[0], spread[1])
    first = math.sqrt(2 / math.pi)
    for i in range(X_STEP):
        for o in range(channels):
            g, c = o // QUAD, o % QUAD
            at = pl.ds((i * groups + g) * y_local, y_local)
            value = total[at, c * NZ : (c + 1) * NZ] + base[o, i]
            inner = value * (first + (first * 0.044715) * (value * value))
            scaled = 0.5 * value
            out[o, i] = (scaled + scaled * jnp.tanh(inner)).astype(out.dtype)


def inverse(place, own, other, base, y_devices, dtype):
    channels, x_local, y_local, _ = base.shape
    z_table, y_table = z_inverse_table(y_devices), y_inverse_table(y_devices)
    whole = pl.BlockSpec(own.shape, lambda x, p: (0, 0, 0))
    cells = pl.BlockSpec((channels, X_STEP, y_local, NZ), lambda x, p: (0, x, 0, 0))
    lines = X_STEP * (channels // QUAD) * y_local
    return pl.pallas_call(
        inverse_kernel,
        out_shape=jax.ShapeDtypeStruct(base.shape, dtype),
        grid_spec=pltpu.PrefetchScalarGridSpec(
            num_scalar_prefetch=1,
            grid=(x_local // X_STEP,),
            in_specs=[
                whole,
                whole,
                cells,
                pl.BlockSpec((1, *y_table.shape[1:]), lambda x, p: (p[0], 0, 0)),
                pl.BlockSpec((1, *z_table.shape[1:]), lambda x, p: (p[0], 0, 0, 0)),
            ],
            out_specs=cells,
            scratch_shapes=[
                pltpu.VMEM((2, 2 * QUAD * MZ, QUAD * NZ), jnp.bfloat16),
                pltpu.VMEM((X_STEP, Y_BLOCKS, LANES, LANES), jnp.float32),
                pltpu.VMEM((X_STEP, Y_BLOCKS, LANES, LANES), jnp.float32),
                pltpu.VMEM((2, lines, 2 * LANES), jnp.bfloat16),
                pltpu.VMEM((lines, QUAD * NZ), jnp.float32),
            ],
        ),
        compiler_params=pltpu.CompilerParams(
            dimension_semantics=("arbitrary",), vmem_limit_bytes=28 * MIB
        ),
        name="inverse",
    )(place, own, other, base, jnp.asarray(y_table), jnp.asarray(z_table))


def spread_weights(spectral_weight):
    m, k = spectral_weight.shape[3:]
    return jnp.pad(spectral_weight, ((0, 0), (0, 0), (0, 0), (0, MP - m), (0, LANES - k)))


def local_matrix(pointwise_weight):
    channels = pointwise_weight.shape[0]
    eye = jnp.eye(MP, dtype=pointwise_weight.dtype)
    matrix = pointwise_weight.T[:, None, :, None] * eye[None, :, None, :]
    return matrix.reshape(channels * MP, channels * MP)


def swapped(x, axis):
    devices = lax.axis_size(axis)
    return lax.ppermute(x, axis, [(d, (d + 1) % devices) for d in range(devices)])


def per_device(field, spectral_weight, pointwise_weight, bias):
    y_devices, x_devices = lax.axis_size("py"), lax.axis_size("px")
    place = lax.axis_index("py").astype(jnp.int32).reshape(1)
    cells = field[0]
    own, other = forward(place, cells, y_devices, x_devices)
    payload = own + swapped(other, "py")
    payload, spectral_weight, pointwise_weight, bias = lax.optimization_barrier(
        (payload, spectral_weight, pointwise_weight, bias)
    )
    received = lax.all_to_all(payload, "px", 0, 0, tiled=True)
    weights = spread_weights(spectral_weight)
    base = pointwise(cells, local_matrix(pointwise_weight), bias)
    received, base = lax.optimization_barrier((received, base))
    result = mix(received, weights)
    own = lax.all_to_all(result, "px", 0, 0, tiled=True)
    other = swapped(own, "py")
    return inverse(place, own, other, base, y_devices, field.dtype)[None]


def solution(mesh):
    in_specs = (
        P("groups", None, "px", "py", None),
        P(None, None, None, ("py", "px"), None),
        P(),
        P(),
    )
    out_specs = P("groups", None, "px", "py", None)
    return jax.shard_map(per_device, mesh=mesh, in_specs=in_specs, out_specs=out_specs, check_vma=False)
```

time: 165 us -> 151 us (0.915)
  Pallas kernels: 32.8 us -> 21 us
  waiting for transfers between devices: 38.7 us -> 32 us
  local copies, waits for them, and re-layouts: 7.19 us -> 12.8 us
    all_to_all x1, waiting for transfers between devices: 36.6 us -> 28.1 us  [per_device(): received = lax.all_to_all(payload, 'px', 0, 0, tiled=True)]
    pallas_call x1, Pallas kernels: 13.9 us -> 5.97 us  [forward(): pl.pallas_call(forward_kernel, out_shape=(payload, payload), grid_spec=pl...]
    unnamed x11 -> x22, local copies, waits for them, and re-layouts: 2.56 us -> 8.08 us
    optimization_barrier x0 -> x1, local copies, waits for them, and re-layouts: none -> 2.46 us  [per_device(): lax.optimization_barrier((payload, spectral_weight, pointwise_weight, bias))]
    pallas_call x1 -> x2, Pallas kernels: 13.3 us -> 11 us  [the longest x1 7.39 us: inverse(): pl.pallas_call(inverse_kernel, out_shape=jax.ShapeDtypeStruct(base.shape,...]
    ppermute x2, waiting for transfers between devices: 2.13 us -> 3.82 us  [swapped(): lax.ppermute(x, axis, [(d, (d + 1) % devices) for d in range(devices)])]
    pad x1, local copies, waits for them, and re-layouts: 2.68 us -> 1 us  [spread_weights(): jnp.pad(spectral_weight, ((0, 0), (0, 0), (0, 0), (0, MP - m), (0, LANES...]
  transfers between devices with their start and end apart: 3 -> 3, of which waited for: 2 -> 3; matrix products, arithmetic and copies ran while one was open for 3% -> 3% of each run, Pallas kernels for 0% -> 2%
where the time goes in v1:
time: 151 us; the launch traced here: 150 us
  blocking collectives  47.6 us (32%)
  starting transfers between devices  35.6 us (24%)
  waiting for transfers between devices  32 us (21%)
  Pallas kernels  21 us (14%)
  local copies, waits for them, and re-layouts  12.8 us (8%)
    all_to_all x1, blocking collectives, per_device(): own = lax.all_to_all(result, 'px', 0, 0, tiled=True)  47.6 us
    all_to_all x1, waiting for transfers between devices, per_device(): received = lax.all_to_all(payload, 'px', 0, 0, tiled=True)  28.1 us
    ppermute x2, starting transfers between devices, swapped(): lax.ppermute(x, axis, [(d, (d + 1) % devices) for d in range(devices)])  25.8 us
    all_to_all x1, starting transfers between devices, per_device(): received = lax.all_to_all(payload, 'px', 0, 0, tiled=True)  9.8 us
    unnamed x22, local copies, waits for them, and re-layouts  8.08 us
    pallas_call x1, Pallas kernels, inverse(): pl.pallas_call(inverse_kernel, out_shape=jax.ShapeDtypeStruct(base.shape,...  7.39 us
    pallas_call x1, Pallas kernels, forward(): pl.pallas_call(forward_kernel, out_shape=(payload, payload), grid_spec=pl...  5.97 us
    pallas_call x1, Pallas kernels, mix(): pl.pallas_call(mix_kernel, out_shape=jax.ShapeDtypeStruct(payload.shape,...  4.06 us
  transfers between devices with their start and end apart: 3, of which 3 were waited for; matrix products, arithmetic and copies ran while one was open for 3% of the time, Pallas kernels for 2%

profile of v1, /device:TPU:33, one launch (start us, length us, event | category | flops | bytes accessed | tf_op | source)
XLA Modules:
  0.0 150.3 jit_solution(11289999469511554881)
XLA Ops:
  0.0 0.0 copy-start.2
  0.0 1.8 %copy-done.2 = bf16[1,20,6,96,128]{4,3,2,1,0:T(8,128)(2,1)S(1)} copy-done((bf16[1,20,6,96,128]{4,3,2,1,0:T(8,128)(2,1)S(1)}, bf16[1,20,6,96,128]{4,3,2,1,0:T(8,128)(2,1)}, u32[]{:S(2)}) %copy-start.2) | copy-done | bytes 2949144
  1.8 0.0 copy-start.7
  1.8 0.9 copy-done.7
  2.8 0.0 copy-start.8
  2.8 0.9 copy-done.8
  3.7 0.0 copy-start.10
  3.7 6.0 %forward.1 = (f32[64,24,128]{2,1,0:T(8,128)S(1)}, f32[64,24,128]{2,1,0:T(8,128)S(1)}) custom-call(s32[1]{0:T(128)} %bitcast.place, bf16[20,6,96,128]{3,2,1,0:T(8,128)(2,1)S(1)} %bitcast.4, bf16[2,2,128,256]{3,2,1,0:T(8,128)(2,1)S(1)} %copy-done.8, bf16[2,256,192]{2,1,0:T(8,128)(2,1)S(1)} %copy-done.7), custom_call_target="tpu_custom_call" | custom-call | tf_op jit(solution)/shard_map/forward/pallas_call | solution.py:177
  9.7 20.5 %collective-permute-start = (f32[64,24,128]{2,1,0:T(8,128)S(1)}, f32[64,24,128]{2,1,0:T(8,128)S(1)}, u32[]{:S(2)}, u32[]{:S(2)}) collective-permute-start(f32[64,24,128]{2,1,0:T(8,128)S(1)} %get-tuple-element.14), channel_id=1, source_target_pairs={{0,1},{1,0},{2,3},{3,2},{4,5},{5,4},{6,7},{7,6},{8,9},{9,8},{10,11... | collective-permute-start | bytes 2359304 | tf_op jit(solution)/shard_map/ppermute | solution.py:396
  30.3 1.9 %collective-permute-done = f32[64,24,128]{2,1,0:T(8,128)S(1)} collective-permute-done((f32[64,24,128]{2,1,0:T(8,128)S(1)}, f32[64,24,128]{2,1,0:T(8,128)S(1)}, u32[]{:S(2)}, u32[]{:S(2)}) %collective-permute-start) | collective-permute-done | bytes 786464 | tf_op jit(solution)/shard_map/ppermute | solution.py:396
  32.2 1.0 add.5
  33.1 9.8 %all-to-all-start = ((f32[64,24,128]{2,1,0:T(8,128)}), f32[64,24,128]{2,1,0:T(8,128)}, u32[]{:S(2)}, u32[]{:S(2)}) async-start(f32[64,24,128]{2,1,0:T(8,128)} %add.5), calls=%async_computation | async-start | bytes 1572864 | tf_op jit(solution)/shard_map/all_to_all | solution.py:408
  43.0 0.0 copy-done.10
  43.0 0.1 copy.12
  43.1 0.2 broadcast_multiply_fusion
  43.3 1.2 mul.20.local
  44.5 2.5 %copy.13 = bf16[2,20,20,12,96]{4,3,2,1,0:T(8,128)(2,1)S(1)} copy(bf16[2,20,20,12,96]{4,0,3,2,1:T(2,128)(2,1)} %param.10) | data formatting | bytes 3686400 | tf_op jit(solution)/shard_map/optimization_barrier | solution.py:405
  46.9 0.0 copy-start.3
  47.0 0.0 copy-start.9
  47.0 1.0 pad.4.weights
  48.0 0.8 copy-done.3
  48.8 0.0 copy-done.9
  48.8 3.6 %pointwise.1.base = f32[20,6,96,128]{3,2,1,0:T(8,128)S(1)} custom-call(bf16[20,6,96,128]{3,2,1,0:T(8,128)(2,1)S(1)} %bitcast.5, bf16[320,320]{1,0:T(8,128)(2,1)S(1)} %mul.20.local, f32[20]{0:T(128)S(1)} %copy-done.9), custom_call_target="tpu_custom_call" | custom-call | flops 943718400 | bytes 8847360 | tf_op jit(solution)/shard_map/pointwise/pallas_call | solution.py:277
  52.4 0.0 copy-start
  52.4 2.5 %copy-done = f32[20,6,96,128]{3,2,1,0:T(8,128)} copy-done((f32[20,6,96,128]{3,2,1,0:T(8,128)}, f32[20,6,96,128]{3,2,1,0:T(8,128)S(1)}, u32[]{:S(2)}) %copy-start) | copy-done | bytes 5898264
  54.9 28.1 %all-to-all-done.payload = f32[64,24,128]{2,1,0:T(8,128)} async-done(((f32[64,24,128]{2,1,0:T(8,128)}), f32[64,24,128]{2,1,0:T(8,128)}, u32[]{:S(2)}, u32[]{:S(2)}) %all-to-all-start) | async-done | bytes 786464 | tf_op jit(solution)/shard_map/all_to_all | solution.py:408
  83.0 0.0 copy-start.5
  83.0 1.0 copy-done.5
  84.0 0.0 copy-start.1
  84.0 0.0 copy-start.4
  84.0 0.0 copy-start.6
  84.0 4.1 %mix.1 = f32[64,24,128]{2,1,0:T(8,128)S(1)} custom-call(f32[64,24,128]{2,1,0:T(8,128)} %all-to-all-done.payload, bf16[2,20,20,16,128]{4,3,2,1,0:T(8,128)(2,1)S(1)} %pad.4.weights, bf16[2,384,256]{2,1,0:T(8,128)(2,1)S(1)} %copy-done.5), custom_call_target="tpu_custom_call" | custom-call | tf_op jit(solution)/shard_map/mix/pallas_call | solution.py:246
  88.1 47.6 %all_to_all.10.own = f32[64,24,128]{2,1,0:T(8,128)S(1)} all-to-all(f32[64,24,128]{2,1,0:T(8,128)S(1)} %mix.1), channel_id=1, replica_groups=mesh['groups'=2,'px'=64,'py'=2] {'px'}, dimensions={0} | all-to-all | bytes 1572864 | tf_op jit(solution)/shard_map/all_to_all | solution.py:413
  135.7 5.3 %collective-permute-start.1 = (f32[64,24,128]{2,1,0:T(8,128)S(1)}, f32[64,24,128]{2,1,0:T(8,128)S(1)}, u32[]{:S(2)}, u32[]{:S(2)}) collective-permute-start(f32[64,24,128]{2,1,0:T(8,128)S(1)} %all_to_all.10.own), channel_id=1, source_target_pairs={{0,1},{1,0},{2,3},{3,2},{4,5},{5,4},{6,7},{7,6},{8,9},{9,8},{10,11... | collective-permute-start | bytes 2359304 | tf_op jit(solution)/shard_map/ppermute | solution.py:396
  141.0 1.9 %collective-permute-done.1.other = f32[64,24,128]{2,1,0:T(8,128)S(1)} collective-permute-done((f32[64,24,128]{2,1,0:T(8,128)S(1)}, f32[64,24,128]{2,1,0:T(8,128)S(1)}, u32[]{:S(2)}, u32[]{:S(2)}) %collective-permute-start.1) | collective-permute-done | bytes 786464 | tf_op jit(solution)/shard_map/ppermute | solution.py:396
  142.9 0.0 copy-done.1
  142.9 0.0 copy-done.4
  142.9 0.0 copy-done.6
  142.9 7.4 %inverse.1 = bf16[20,6,96,128]{3,2,1,0:T(8,128)(2,1)} custom-call(s32[1]{0:T(128)} %bitcast.place, f32[64,24,128]{2,1,0:T(8,128)S(1)} %all_to_all.10.own, f32[64,24,128]{2,1,0:T(8,128)S(1)} %collective-permute-done.1.other, f32[20,6,96,128]{3,2,1,0:T(8,128)S(1)} %copy-done.1, bf16[2,384,256]{2,1,0:T(8,128)(2,1)S(1)} %copy-done.4, ...), custom_call_target="tpu_custom_call" | custom-call | tf_op jit(solution)/shard_map/inverse/pallas_call | solution.py:353
  (1 shorter events, 0.0 us)
Async XLA Ops:
  0.0 1.8 %copy-start.2 = (bf16[1,20,6,96,128]{4,3,2,1,0:T(8,128)(2,1)S(1)}, bf16[1,20,6,96,128]{4,3,2,1,0:T(8,128)(2,1)}, u32[]{:S(2)}) copy-start(bf16[1,20,6,96,128]{4,3,2,1,0:T(8,128)(2,1)} %param.9) | copy-start | bytes 8847364
  1.8 0.9 copy-start.7
  2.8 0.9 copy-start.8
  3.7 39.2 %copy-start.10 = (bf16[20,20]{1,0:T(8,128)(2,1)S(1)}, bf16[20,20]{1,0:T(8,128)(2,1)}, u32[]{:S(2)}) copy-start(bf16[20,20]{1,0:T(8,128)(2,1)} %param.11) | copy-start | bytes 2404
  9.7 22.4 %collective-permute-start = (f32[64,24,128]{2,1,0:T(8,128)S(1)}, f32[64,24,128]{2,1,0:T(8,128)S(1)}, u32[]{:S(2)}, u32[]{:S(2)}) collective-permute-start(f32[64,24,128]{2,1,0:T(8,128)S(1)} %get-tuple-element.14), channel_id=1, source_target_pairs={{0,1},{1,0},{2,3},{3,2},{4,5},{5,4},{6,7},{7,6},{8,9},{9,8},{10,11... | collective-permute-start | bytes 2359304 | tf_op jit(solution)/shard_map/ppermute | solution.py:396
  33.1 49.9 %all-to-all-start = ((f32[64,24,128]{2,1,0:T(8,128)}), f32[64,24,128]{2,1,0:T(8,128)}, u32[]{:S(2)}, u32[]{:S(2)}) async-start(f32[64,24,128]{2,1,0:T(8,128)} %add.5), calls=%async_computation | async-start | bytes 1572864 | tf_op jit(solution)/shard_map/all_to_all | solution.py:408
  46.9 1.8 %copy-start.3 = (bf16[1,20,6,96,128]{4,3,2,1,0:T(8,128)(2,1)S(1)}, bf16[1,20,6,96,128]{4,3,2,1,0:T(8,128)(2,1)}, u32[]{:S(2)}) copy-start(bf16[1,20,6,96,128]{4,3,2,1,0:T(8,128)(2,1)} %param.9) | copy-start | bytes 8847364
  47.0 1.8 %copy-start.9 = (f32[20]{0:T(128)S(1)}, f32[20]{0:T(128)}, u32[]{:S(2)}) copy-start(f32[20]{0:T(128)} %bias) | copy-start | bytes 244
  52.4 2.5 %copy-start = (f32[20,6,96,128]{3,2,1,0:T(8,128)}, f32[20,6,96,128]{3,2,1,0:T(8,128)S(1)}, u32[]{:S(2)}) copy-start(f32[20,6,96,128]{3,2,1,0:T(8,128)S(1)} %pointwise.1.base) | copy-start | bytes 17694724
  83.0 1.0 copy-start.5
  84.0 58.9 %copy-start.1 = (f32[20,6,96,128]{3,2,1,0:T(8,128)S(1)}, f32[20,6,96,128]{3,2,1,0:T(8,128)}, u32[]{:S(2)}) copy-start(f32[20,6,96,128]{3,2,1,0:T(8,128)} %copy-done) | copy-start | bytes 17694724
  84.0 58.9 %copy-start.4 = (bf16[2,384,256]{2,1,0:T(8,128)(2,1)S(1)}, bf16[2,384,256]{2,1,0:T(8,128)(2,1)}, u32[]{:S(2)}) copy-start(bf16[2,384,256]{2,1,0:T(8,128)(2,1)} %constant.20.clone.y_table) | copy-start | bytes 1179652
  84.0 58.9 %copy-start.6 = (bf16[2,2,256,128]{3,2,1,0:T(8,128)(2,1)S(1)}, bf16[2,2,256,128]{3,2,1,0:T(8,128)(2,1)}, u32[]{:S(2)}) copy-start(bf16[2,2,256,128]{3,2,1,0:T(8,128)(2,1)} %constant.21.clone.z_table) | copy-start | bytes 786436
  135.7 7.2 %collective-permute-start.1 = (f32[64,24,128]{2,1,0:T(8,128)S(1)}, f32[64,24,128]{2,1,0:T(8,128)S(1)}, u32[]{:S(2)}, u32[]{:S(2)}) collective-permute-start(f32[64,24,128]{2,1,0:T(8,128)S(1)} %all_to_all.10.own), channel_id=1, source_target_pairs={{0,1},{1,0},{2,3},{3,2},{4,5},{5,4},{6,7},{7,6},{8,9},{9,8},{10,11... | collective-permute-start | bytes 2359304 | tf_op jit(solution)/shard_map/ppermute | solution.py:396

commit v2 on v1

v2 whole, which is shorter than its diff:
```python
import functools
import math

import jax
import jax.numpy as jnp
import numpy as np
from jax import lax
from jax.experimental import pallas as pl
from jax.experimental.pallas import tpu as pltpu
from jax.sharding import PartitionSpec as P

NX = 384
NY = 192
NZ = 128
MX = 96
MY = 48
MZ = 32

LANES = 128
QUAD = 4
Y_BLOCKS = 4
M = MY // Y_BLOCKS
MP = 16
HALF = 64
SPARE = 4
X_FORWARD = 3
X_INVERSE = 2
MIB = 1024 * 1024


def kept(length, retained):
    index = np.arange(retained)
    return np.where(index < retained // 2, index, length - retained + index)


def angles(frequency, positions, length):
    return 2 * np.pi * ((frequency[:, None] * positions[None, :]) % length) / length


def halves(table):
    high = table.astype(np.float32).astype(jnp.bfloat16)
    low = (table - high.astype(np.float64)).astype(np.float32).astype(jnp.bfloat16)
    return np.stack([high, low])


def split(value):
    high = value.astype(jnp.bfloat16)
    low = (value - high.astype(jnp.float32)).astype(jnp.bfloat16)
    return high, low


def in_hbm(array):
    return pltpu.with_memory_space_constraint(array, pltpu.HBM)


def dot(a, b, contract=((1,), (0,))):
    return lax.dot_general(a, b, (contract, ((), ())), preferred_element_type=jnp.float32)


def z_order(y_devices):
    order = np.arange(MZ).reshape(y_devices, MZ // y_devices)
    return [np.concatenate([order[d], np.delete(order, d, 0).reshape(-1)]) for d in range(y_devices)]


def z_forward_table(y_devices):
    tables = []
    for kz in z_order(y_devices):
        angle = np.tile(angles(kz, np.arange(NZ), NZ).T, (1, QUAD))
        tables.append(halves(np.concatenate([np.cos(angle), -np.sin(angle)], 1)))
    return np.stack(tables)


def stacked(table):
    high, low = halves(table)
    return np.concatenate([np.concatenate([high, high], 1), np.concatenate([low, np.zeros_like(low)], 1)], 0)


def y_forward_table(y_devices):
    tables = []
    rows = NY // y_devices
    for d in range(y_devices):
        angle = angles(kept(NY, MY), d * rows + np.arange(rows), NY)
        table = np.zeros((2, Y_BLOCKS, MP, rows))
        table[0, :, :M] = np.cos(angle).reshape(Y_BLOCKS, M, rows)
        table[1, :, :M] = np.sin(angle).reshape(Y_BLOCKS, M, rows)
        tables.append(stacked(table.reshape(2 * Y_BLOCKS * MP, rows)))
    return np.stack(tables)


def x_table(x_local):
    angle = angles(kept(NX, MX), np.arange(NX).reshape(-1, x_local).T.reshape(-1), NX).T
    table = np.zeros((NX, 2, LANES))
    table[:, 0, :MX] = np.cos(angle)
    table[:, 1, :MX] = np.sin(angle)
    return halves(table.reshape(NX, 2 * LANES))


def y_inverse_table(y_devices):
    tables = []
    rows = NY // y_devices
    for d in range(y_devices):
        angle = angles(kept(NY, MY), d * rows + np.arange(rows), NY).T
        table = np.zeros((2, rows, 2, Y_BLOCKS, MP))
        cosine = np.cos(angle).reshape(rows, Y_BLOCKS, M)
        sine = np.sin(angle).reshape(rows, Y_BLOCKS, M)
        table[0, :, 0, :, :M] = cosine
        table[0, :, 1, :, :M] = -sine
        table[1, :, 0, :, :M] = sine
        table[1, :, 1, :, :M] = cosine
        tables.append(stacked(table.reshape(2 * rows, 2 * Y_BLOCKS * MP)))
    return np.stack(tables)


def z_inverse_table(y_devices):
    tables = []
    for kz in z_order(y_devices):
        angle = angles(kz, np.arange(NZ), NZ)
        weight = np.where(kz == 0, 1.0, 2.0)[:, None] / (NX * NY * NZ)
        cosine = np.tile(np.cos(angle) * weight, (QUAD, 1))
        sine = np.tile(np.sin(angle) * weight, (QUAD, 1))
        tables.append(halves(np.concatenate([cosine, -sine], 0)))
    return np.stack(tables)


def own_block(table, c, dim):
    at = lax.broadcasted_iota(jnp.int32, table.shape, dim) // MZ % QUAD
    return jnp.where(at == c, table.astype(jnp.float32), 0.0).astype(jnp.bfloat16)


def lane_of_part(shape):
    return lax.broadcasted_iota(jnp.int32, shape, len(shape) - 1) % HALF


def with_spare(row, value, last):
    used = HALF - SPARE
    if row >= used // SPARE:
        return value
    moved = pltpu.roll(last, used - SPARE * row, 1)
    return jnp.where(lane_of_part(value.shape) >= used, moved, value)


def last_row(value_of_row):
    used = HALF - SPARE
    result = value_of_row(0)
    at = lane_of_part(result.shape) // SPARE
    result = pltpu.roll(result, LANES - used, 1)
    for row in range(1, used // SPARE):
        moved = pltpu.roll(value_of_row(row), LANES - used + SPARE * row, 1)
        result = jnp.where(at == row, moved, result)
    return result


def forward_kernel(
    x_local, place, field, z_tables, y_tables, own, other, cells, z_table, y_table, spread, z_hat, rows, loaded
):
    channels, _, y_local, _ = field.shape
    groups = channels // QUAD
    per_x = QUAD * MZ
    half = MZ // 2
    size = Y_BLOCKS * MP
    sent = x_local * QUAD - 1
    order = list(range(x_local))[::-1]
    loads = [pltpu.make_async_copy(field.at[:, x], cells.at[x], loaded.at[x]) for x in range(x_local)]
    tables = [
        pltpu.make_async_copy(z_tables.at[place[0]], z_table, loaded.at[x_local]),
        pltpu.make_async_copy(y_tables.at[place[0]], y_table, loaded.at[x_local + 1]),
    ]
    tables[0].start()
    for x in order[:X_FORWARD]:
        loads[x].start()
    tables[1].start()
    for x in order[X_FORWARD:]:
        loads[x].start()
    tables[0].wait()
    for part in range(2):
        for c in range(QUAD):
            spread[part, c * NZ : (c + 1) * NZ, :] = own_block(z_table[part], c, 1)
    last = {}
    for first in range(0, x_local, X_FORWARD):
        chunk = order[first : first + X_FORWARD]
        for x in chunk:
            loads[x].wait()
        inputs = jnp.concatenate(
            [
                jnp.concatenate([cells[x, QUAD * g + c] for c in range(QUAD)], 1)
                for x in chunk
                for g in range(groups)
            ],
            0,
        )
        z_hat[first // X_FORWARD] = dot(inputs, spread[0]) + dot(inputs, spread[1])
        if first == 0:
            tables[1].wait()
        for i, x in enumerate(chunk):
            for g in range(groups):
                at = pl.ds((i * groups + g) * y_local, y_local)
                high, low = split(z_hat[first // X_FORWARD, at, :])
                parts = dot(y_table[...], jnp.concatenate([high, low], 0))
                parts = parts[: 2 * size] + parts[2 * size :]
                real = parts[:size, :per_x] + parts[size:, per_x:]
                imag = parts[:size, per_x:] - parts[size:, :per_x]
                for block in range(Y_BLOCKS):
                    for s, value in enumerate((real, imag)):
                        at = pl.ds(s * HALF + g * M, MP)
                        rows[x, block, at, :] = value[block * MP : (block + 1) * MP]
            for block in range(Y_BLOCKS):
                turned = rows[x, block, :LANES, :].T
                for c in reversed(range(QUAD)):
                    row = x * QUAD + c
                    for k, out in enumerate((own, other)):
                        value = turned[c * MZ + k * half : c * MZ + (k + 1) * half]
                        if row == sent:
                            last[block, k] = value
                        else:
                            at = pl.ds(block * sent + row, half, stride=Y_BLOCKS * sent)
                            out[at, :] = with_spare(row, value, last[block, k])


def forward(place, field, y_devices, x_devices):
    channels, x_local, y_local, _ = field.shape
    z_table, y_table = z_forward_table(y_devices), y_forward_table(y_devices)
    payload = jax.ShapeDtypeStruct((x_devices * (x_local * QUAD - 1), LANES), jnp.float32)
    lines = X_FORWARD * (channels // QUAD) * y_local
    vmem = pl.BlockSpec(memory_space=pltpu.VMEM)
    return pl.pallas_call(
        functools.partial(forward_kernel, x_local),
        out_shape=(payload, payload),
        grid_spec=pltpu.PrefetchScalarGridSpec(
            num_scalar_prefetch=1,
            grid=(1,),
            in_specs=[pl.BlockSpec(memory_space=pltpu.HBM)] * 3,
            out_specs=[vmem, vmem],
            scratch_shapes=[
                pltpu.VMEM((x_local, channels, y_local, NZ), field.dtype),
                pltpu.VMEM(z_table.shape[1:], jnp.bfloat16),
                pltpu.VMEM(y_table.shape[1:], jnp.bfloat16),
                pltpu.VMEM((2, QUAD * NZ, 2 * QUAD * MZ), jnp.bfloat16),
                pltpu.VMEM((x_local // X_FORWARD, lines, 2 * QUAD * MZ), jnp.float32),
                pltpu.VMEM((x_local, Y_BLOCKS, LANES + MP, LANES), jnp.float32),
                pltpu.SemaphoreType.DMA((x_local + 2,)),
            ],
        ),
        compiler_params=pltpu.CompilerParams(
            dimension_semantics=("arbitrary",), vmem_limit_bytes=24 * MIB
        ),
        name="forward",
    )(place, in_hbm(field), in_hbm(jnp.asarray(z_table)), in_hbm(jnp.asarray(y_table)))


def mix_kernel(x_local, payload, weights, table_hbm, result, table, spectrum, mixed, done):
    channels = weights.shape[1]
    sent = x_local * QUAD - 1
    x_devices = payload.shape[0] // sent
    load = pltpu.make_async_copy(table_hbm, table, done)
    load.start()

    def row_of(row):
        return pl.ds(row, x_devices, stride=sent)

    lines = [payload[row_of(row), :] for row in range(sent)]
    lines.append(last_row(lambda row: lines[row]))
    rows = jnp.concatenate([jnp.concatenate(lines[c::QUAD], 0) for c in range(QUAD)], 1)
    high, low = split(rows.T)
    load.wait()
    parts = dot(high, table[0]) + dot(low, table[0]) + dot(high, table[1])
    for c in range(QUAD):
        upper = parts[c * LANES : c * LANES + HALF]
        lower = parts[c * LANES + HALF : (c + 1) * LANES]
        spectrum[c, 0] = upper[:, :LANES] + lower[:, LANES:]
        spectrum[c, 1] = lower[:, :LANES] - upper[:, LANES:]
    outs = channels // 2
    for first in range(0, channels, outs):
        real = [jnp.zeros((MP, LANES), jnp.float32)] * outs
        imag = [jnp.zeros((MP, LANES), jnp.float32)] * outs
        for i in range(channels):
            g, c = i // QUAD, i % QUAD
            real_in = spectrum[c, 0, pl.ds(g * M, MP), :]
            imag_in = spectrum[c, 1, pl.ds(g * M, MP), :]
            for k in range(outs):
                w_real = weights[0, i, first + k].astype(jnp.float32)
                w_imag = weights[1, i, first + k].astype(jnp.float32)
                real[k] = real[k] + (w_real * real_in - w_imag * imag_in)
                imag[k] = imag[k] + (w_real * imag_in + w_imag * real_in)
        for k in range(outs):
            g, c = (first + k) // QUAD, (first + k) % QUAD
            upper = pl.ds(g * M, MP)
            lower = pl.ds(HALF + g * M, MP)
            mixed[c, upper, :LANES] = real[k]
            mixed[c, upper, LANES:] = -imag[k]
            mixed[c, lower, :LANES] = imag[k]
            mixed[c, lower, LANES:] = real[k]
    last = None
    for c in range(QUAD - 2, -1, -2):
        high, low = split(jnp.concatenate([mixed[c, :LANES, :], mixed[c + 1, :LANES, :]], 0))
        over_k = ((1,), (1,))
        back = dot(table[0], high, over_k) + dot(table[0], low, over_k) + dot(table[1], high, over_k)
        if last is None:
            last = back[(x_local - 1) * x_devices :, LANES:]
        for x in range(x_local):
            for k in range(2):
                row = x * QUAD + c + k
                if row < sent:
                    value = back[x * x_devices : (x + 1) * x_devices, k * LANES : (k + 1) * LANES]
                    result[row_of(row), :] = with_spare(row, value, last)


def mix(payload, weights, x_local):
    table = x_table(x_local)
    vmem = pl.BlockSpec(memory_space=pltpu.VMEM)
    return pl.pallas_call(
        functools.partial(mix_kernel, x_local),
        out_shape=jax.ShapeDtypeStruct(payload.shape, jnp.float32),
        in_specs=[vmem, vmem, pl.BlockSpec(memory_space=pltpu.HBM)],
        out_specs=vmem,
        scratch_shapes=[
            pltpu.VMEM(table.shape, jnp.bfloat16),
            pltpu.VMEM((QUAD, 2, HALF, LANES), jnp.float32),
            pltpu.VMEM((QUAD, LANES + MP, 2 * LANES), jnp.float32),
            pltpu.SemaphoreType.DMA,
        ],
        compiler_params=pltpu.CompilerParams(vmem_limit_bytes=20 * MIB),
        name="mix",
    )(payload, weights, in_hbm(jnp.asarray(table)))


def pointwise_kernel(field, local, bias, out):
    channels, steps, y_local, _ = field.shape
    for i in range(steps):
        for y in range(0, y_local, 2 * MP):
            pair = [
                field[:, i, y + j * MP : y + (j + 1) * MP, :].reshape(channels * MP, NZ) for j in range(2)
            ]
            mixed = dot(local[...], jnp.concatenate(pair, 1))
            for o in range(channels):
                for j in range(2):
                    value = mixed[o * MP : (o + 1) * MP, j * NZ : (j + 1) * NZ]
                    out[o, i, y + j * MP : y + (j + 1) * MP, :] = value + bias[o]


def pointwise(field, local, bias):
    channels, x_local, y_local, _ = field.shape
    cells = pl.BlockSpec((channels, 1, y_local, NZ), lambda x: (0, x, 0, 0))
    return pl.pallas_call(
        pointwise_kernel,
        out_shape=jax.ShapeDtypeStruct(field.shape, jnp.float32),
        grid=(x_local,),
        in_specs=[cells, pl.BlockSpec(local.shape, lambda x: (0, 0)), pl.BlockSpec(memory_space=pltpu.SMEM)],
        out_specs=cells,
        compiler_params=pltpu.CompilerParams(
            dimension_semantics=("arbitrary",), vmem_limit_bytes=12 * MIB
        ),
        cost_estimate=pl.CostEstimate(
            flops=2 * field.size * channels * MP, transcendentals=0, bytes_accessed=6 * field.size
        ),
        name="pointwise",
    )(field, local, bias)


def inverse_kernel(place, own, other, base, y_table, z_table, out, spread, rows, modes, lines, total, cells, stored):
    del place
    channels, x_local, y_local, _ = base.shape
    groups = channels // QUAD
    half = MZ // 2
    sent = x_local * QUAD - 1
    for part in range(2):
        for c in range(QUAD):
            spread[part, :, c * NZ : (c + 1) * NZ] = own_block(z_table[0, part], c, 0)

    def row_of(block, row):
        return pl.ds(block * sent + row, half, stride=Y_BLOCKS * sent)

    stores = [pltpu.make_async_copy(cells.at[x], out.at[:, x], stored.at[x]) for x in range(x_local)]
    for first in range(0, x_local, X_INVERSE):
        chunk = range(first, first + X_INVERSE)
        for x in chunk:
            for block in range(Y_BLOCKS):
                for c in range(QUAD):
                    for k, source in enumerate((own, other)):
                        row = x * QUAD + c
                        if row < sent:
                            value = source[row_of(block, row), :]
                        else:
                            value = last_row(lambda r: source[row_of(block, r), :])
                        rows[x, block, c * MZ + k * half : c * MZ + (k + 1) * half] = value
                modes[x, block] = rows[x, block].T
        for g in range(groups):
            inputs = jnp.concatenate(
                [
                    jnp.concatenate([modes[x, block, pl.ds(s * HALF + g * M, MP), :] for x in chunk], 1)
                    for s in range(2)
                    for block in range(Y_BLOCKS)
                ],
                0,
            )
            high, low = split(inputs)
            parts = dot(y_table[0], jnp.concatenate([high, low], 0))
            parts = parts[: 2 * y_local] + parts[2 * y_local :]
            for i in range(X_INVERSE):
                at = pl.ds(((first + i) * groups + g) * y_local, y_local)
                for s in range(2):
                    high, low = split(parts[s * y_local : (s + 1) * y_local, i * LANES : (i + 1) * LANES])
                    lines[0, at, s * LANES : (s + 1) * LANES] = high
                    lines[1, at, s * LANES : (s + 1) * LANES] = low
        at = pl.ds(first * groups * y_local, X_INVERSE * groups * y_local)
        high, low = lines[0, at, :], lines[1, at, :]
        total[at, :] = dot(high, spread[0]) + dot(low, spread[0]) + dot(high, spread[1])
        scale = math.sqrt(2 / math.pi)
        for x in chunk:
            for o in range(channels):
                g, c = o // QUAD, o % QUAD
                at = pl.ds((x * groups + g) * y_local, y_local)
                value = total[at, c * NZ : (c + 1) * NZ] + base[o, x]
                inner = value * (scale + (scale * 0.044715) * (value * value))
                scaled = 0.5 * value
                cells[x, o] = (scaled + scaled * jnp.tanh(inner)).astype(out.dtype)
            stores[x].start()
    for store in stores:
        store.wait()


def inverse(place, own, other, base, y_devices, dtype):
    channels, x_local, y_local, _ = base.shape
    z_table, y_table = z_inverse_table(y_devices), y_inverse_table(y_devices)
    vmem = pl.BlockSpec(memory_space=pltpu.VMEM)
    lines = x_local * (channels // QUAD) * y_local
    return pl.pallas_call(
        inverse_kernel,
        out_shape=jax.ShapeDtypeStruct(base.shape, dtype),
        grid_spec=pltpu.PrefetchScalarGridSpec(
            num_scalar_prefetch=1,
            grid=(1,),
            in_specs=[
                vmem,
                vmem,
                vmem,
                pl.BlockSpec((1, *y_table.shape[1:]), lambda x, p: (p[0], 0, 0)),
                pl.BlockSpec((1, *z_table.shape[1:]), lambda x, p: (p[0], 0, 0, 0)),
            ],
            out_specs=pl.BlockSpec(memory_space=pltpu.HBM),
            scratch_shapes=[
                pltpu.VMEM((2, 2 * QUAD * MZ, QUAD * NZ), jnp.bfloat16),
                pltpu.VMEM((x_local, Y_BLOCKS, LANES, LANES), jnp.float32),
                pltpu.VMEM((x_local, Y_BLOCKS, LANES, LANES), jnp.float32),
                pltpu.VMEM((2, lines, 2 * LANES), jnp.bfloat16),
                pltpu.VMEM((lines, QUAD * NZ), jnp.float32),
                pltpu.VMEM((x_local, channels, y_local, NZ), dtype),
                pltpu.SemaphoreType.DMA((x_local,)),
            ],
        ),
        compiler_params=pltpu.CompilerParams(
            dimension_semantics=("arbitrary",), vmem_limit_bytes=36 * MIB
        ),
        name="inverse",
    )(place, own, other, base, jnp.asarray(y_table), jnp.asarray(z_table))


def spread_weights(spectral_weight):
    m, k = spectral_weight.shape[3:]
    return jnp.pad(spectral_weight, ((0, 0), (0, 0), (0, 0), (0, MP - m), (0, LANES - k)))


def local_matrix(pointwise_weight):
    channels = pointwise_weight.shape[0]
    eye = jnp.eye(MP, dtype=pointwise_weight.dtype)
    matrix = pointwise_weight.T[:, None, :, None] * eye[None, :, None, :]
    return matrix.reshape(channels * MP, channels * MP)


def swapped(x, axis):
    devices = lax.axis_size(axis)
    return lax.ppermute(x, axis, [(d, (d + 1) % devices) for d in range(devices)])


def exchanged(rows, axis):
    devices = lax.axis_size(axis)
    blocks = rows.reshape(devices, rows.shape[0] // devices, 1, LANES)
    return lax.all_to_all(blocks, axis, 0, 0, tiled=True).reshape(rows.shape)


def per_device(field, spectral_weight, pointwise_weight, bias):
    y_devices, x_devices = lax.axis_size("py"), lax.axis_size("px")
    place = lax.axis_index("py").astype(jnp.int32).reshape(1)
    cells = field[0]
    own, other = forward(place, cells, y_devices, x_devices)
    payload = own + swapped(other, "py")
    payload, spectral_weight, pointwise_weight, bias = lax.optimization_barrier(
        (payload, spectral_weight, pointwise_weight, bias)
    )
    received = exchanged(payload, "px")
    weights = spread_weights(spectral_weight)
    base = pointwise(cells, local_matrix(pointwise_weight), bias)
    received, base = lax.optimization_barrier((received, base))
    result = mix(received, weights, cells.shape[1])
    own = exchanged(result, "px")
    other = swapped(own, "py")
    return inverse(place, own, other, base, y_devices, field.dtype)[None]


def solution(mesh):
    in_specs = (
        P("groups", None, "px", "py", None),
        P(None, None, None, ("py", "px"), None),
        P(),
        P(),
    )
    out_specs = P("groups", None, "px", "py", None)
    return jax.shard_map(per_device, mesh=mesh, in_specs=in_specs, out_specs=out_specs, check_vma=False)
```

time: 151 us -> 144 us (0.954)
  local copies, waits for them, and re-layouts: 12.8 us -> 8.13 us
  waiting for transfers between devices: 32 us -> 30.4 us
    unnamed x22 -> x14, local copies, waits for them, and re-layouts: 8.08 us -> 3.37 us
    pallas_call x2, Pallas kernels: 10 us -> 12.7 us  [the longest x1 7.13 us: forward(): pl.pallas_call(functools.partial(forward_kernel, x_local), out_shape=(pay...]
    pallas_call x1, Pallas kernels: 7.39 us -> 5.67 us  [inverse(): pl.pallas_call(inverse_kernel, out_shape=jax.ShapeDtypeStruct(base.shape,...]
where the time goes in v2:
time: 144 us
  blocking collectives  46.2 us (32%)
  starting transfers between devices  35.7 us (25%)
  waiting for transfers between devices  30.4 us (21%)
  Pallas kernels  22 us (15%)
  local copies, waits for them, and re-layouts  8.13 us (6%)
    all_to_all x1, blocking collectives, exchanged(): return lax.all_to_all(blocks, axis, 0, 0, tiled=True).reshape(rows.shape)  46.2 us
    all_to_all x1, waiting for transfers between devices, exchanged(): return lax.all_to_all(blocks, axis, 0, 0, tiled=True).reshape(rows.shape)  26.7 us
    ppermute x2, starting transfers between devices, swapped(): lax.ppermute(x, axis, [(d, (d + 1) % devices) for d in range(devices)])  25.9 us
    all_to_all x1, starting transfers between devices, exchanged(): return lax.all_to_all(blocks, axis, 0, 0, tiled=True).reshape(rows.shape)  9.81 us
    pallas_call x1, Pallas kernels, forward(): pl.pallas_call(functools.partial(forward_kernel, x_local), out_shape=(pay...  7.13 us
    pallas_call x1, Pallas kernels, inverse(): pl.pallas_call(inverse_kernel, out_shape=jax.ShapeDtypeStruct(base.shape,...  5.67 us
    pallas_call x1, Pallas kernels, mix(): pl.pallas_call(functools.partial(mix_kernel, x_local), out_shape=jax.Shap...  5.61 us
    ppermute x2, waiting for transfers between devices, swapped(): lax.ppermute(x, axis, [(d, (d + 1) % devices) for d in range(devices)])  3.73 us
  transfers between devices with their start and end apart: 3, of which 3 were waited for; matrix products, arithmetic and copies ran while one was open for 3% of the time, Pallas kernels for 2%

profile of v2, /device:TPU:33, one launch (start us, length us, event | category | flops | bytes accessed | tf_op | source)
XLA Modules:
  0.0 143.9 jit_solution(4474934547199072848)
XLA Ops:
  0.0 0.0 copy-start.6
  0.0 7.1 %forward.1 = (f32[1472,128]{1,0:T(8,128)S(1)}, f32[1472,128]{1,0:T(8,128)S(1)}) custom-call(s32[1]{0:T(128)} %bitcast.place, bf16[20,6,96,128]{3,2,1,0:T(8,128)(2,1)} %bitcast.8, bf16[2,2,128,256]{3,2,1,0:T(8,128)(2,1)} %constant.17.clone.z_tables, bf16[2,256,192]{2,1,0:T(8,128)(2,1)} %constant.18.clone.y_tables), custom_call_target="tpu_custom_call" | custom-call | tf_op jit(solution)/shard_map/forward/pallas_call | solution.py:225
  7.1 20.5 %collective-permute-start = (f32[1472,128]{1,0:T(8,128)S(1)}, f32[1472,128]{1,0:T(8,128)S(1)}, u32[]{:S(2)}, u32[]{:S(2)}) collective-permute-start(f32[1472,128]{1,0:T(8,128)S(1)} %get-tuple-element.14), channel_id=1, source_target_pairs={{0,1},{1,0},{2,3},{3,2},{4,5},{5,4},{6,7},{7,6},{8,9},{9,8},{10,11... | collective-permute-start | bytes 2261000 | tf_op jit(solution)/shard_map/ppermute | solution.py:471
  27.7 1.9 %collective-permute-done = f32[1472,128]{1,0:T(8,128)S(1)} collective-permute-done((f32[1472,128]{1,0:T(8,128)S(1)}, f32[1472,128]{1,0:T(8,128)S(1)}, u32[]{:S(2)}, u32[]{:S(2)}) %collective-permute-start) | collective-permute-done | bytes 753696 | tf_op jit(solution)/shard_map/ppermute | solution.py:471
  29.5 0.9 add.5
  30.5 9.8 %all-to-all-start = ((f32[64,23,1,128]{3,2,1,0:T(1,128)}), f32[64,23,1,128]{3,2,1,0:T(1,128)}, u32[]{:S(2)}, u32[]{:S(2)}) async-start(f32[64,23,1,128]{3,2,1,0:T(1,128)} %bitcast.2), calls=%async_computation | async-start | bytes 1507328 | tf_op jit(solution)/shard_map/all_to_all | solution.py:477
  40.3 0.0 copy-done.6
  40.3 0.1 copy.15
  40.4 0.2 broadcast_multiply_fusion
  40.6 1.2 mul.20.local
  41.8 2.5 %copy.16 = bf16[2,20,20,12,96]{4,3,2,1,0:T(8,128)(2,1)S(1)} copy(bf16[2,20,20,12,96]{4,0,3,2,1:T(2,128)(2,1)} %param.10) | data formatting | bytes 3686400 | tf_op jit(solution)/shard_map/optimization_barrier | solution.py:486
  44.3 0.0 copy-start.2
  44.3 0.0 copy-start.5
  44.3 1.0 pad.4.weights
  45.3 0.8 copy-done.2
  46.1 0.0 copy-done.5
  46.1 3.6 %pointwise.1.base = f32[20,6,96,128]{3,2,1,0:T(8,128)S(1)} custom-call(bf16[20,6,96,128]{3,2,1,0:T(8,128)(2,1)S(1)} %bitcast.9, bf16[320,320]{1,0:T(8,128)(2,1)S(1)} %mul.20.local, f32[20]{0:T(128)S(1)} %copy-done.5), custom_call_target="tpu_custom_call" | custom-call | flops 943718400 | bytes 8847360 | tf_op jit(solution)/shard_map/pointwise/pallas_call | solution.py:343
  49.7 0.0 copy-start
  49.7 2.5 %copy-done = f32[20,6,96,128]{3,2,1,0:T(8,128)} copy-done((f32[20,6,96,128]{3,2,1,0:T(8,128)}, f32[20,6,96,128]{3,2,1,0:T(8,128)S(1)}, u32[]{:S(2)}) %copy-start) | copy-done | bytes 5898264
  52.3 26.7 %all-to-all-done = f32[64,23,1,128]{3,2,1,0:T(1,128)} async-done(((f32[64,23,1,128]{3,2,1,0:T(1,128)}), f32[64,23,1,128]{3,2,1,0:T(1,128)}, u32[]{:S(2)}, u32[]{:S(2)}) %all-to-all-start) | async-done | bytes 753696 | tf_op jit(solution)/shard_map/all_to_all | solution.py:477
  79.0 0.0 copy-start.1
  79.0 0.0 copy-start.3
  79.0 0.0 copy-start.4
  79.0 5.6 %mix.1 = f32[1472,128]{1,0:T(8,128)S(1)} custom-call(f32[1472,128]{1,0:T(8,128)} %bitcast.3.payload, bf16[2,20,20,16,128]{4,3,2,1,0:T(8,128)(2,1)S(1)} %pad.4.weights, bf16[2,384,256]{2,1,0:T(8,128)(2,1)} %constant.19.clone.table_hbm), custom_call_target="tpu_custom_call" | custom-call | tf_op jit(solution)/shard_map/mix/pallas_call | solution.py:310
  84.6 46.2 %all_to_all.10 = f32[64,23,1,128]{3,2,1,0:T(1,128)S(1)} all-to-all(f32[64,23,1,128]{3,2,1,0:T(1,128)S(1)} %bitcast.10), channel_id=1, replica_groups=mesh['groups'=2,'px'=64,'py'=2] {'px'}, dimensions={0} | all-to-all | bytes 1507328 | tf_op jit(solution)/shard_map/all_to_all | solution.py:477
  130.9 5.4 %collective-permute-start.1 = (f32[1472,128]{1,0:T(8,128)S(1)}, f32[1472,128]{1,0:T(8,128)S(1)}, u32[]{:S(2)}, u32[]{:S(2)}) collective-permute-start(f32[1472,128]{1,0:T(8,128)S(1)} %bitcast.11), channel_id=1, source_target_pairs={{0,1},{1,0},{2,3},{3,2},{4,5},{5,4},{6,7},{7,6},{8,9},{9,8},{10,11... | collective-permute-start | bytes 2261000 | tf_op jit(solution)/shard_map/ppermute | solution.py:471
  136.2 1.9 %collective-permute-done.1.other = f32[1472,128]{1,0:T(8,128)S(1)} collective-permute-done((f32[1472,128]{1,0:T(8,128)S(1)}, f32[1472,128]{1,0:T(8,128)S(1)}, u32[]{:S(2)}, u32[]{:S(2)}) %collective-permute-start.1) | collective-permute-done | bytes 753696 | tf_op jit(solution)/shard_map/ppermute | solution.py:471
  138.1 0.0 copy-done.1
  138.1 0.0 copy-done.3
  138.1 0.0 copy-done.4
  138.1 5.7 %inverse.1 = bf16[20,6,96,128]{3,2,1,0:T(8,128)(2,1)} custom-call(s32[1]{0:T(128)} %bitcast.place, f32[1472,128]{1,0:T(8,128)S(1)} %bitcast.12, f32[1472,128]{1,0:T(8,128)S(1)} %collective-permute-done.1.other, f32[20,6,96,128]{3,2,1,0:T(8,128)S(1)} %copy-done.1, bf16[2,384,256]{2,1,0:T(8,128)(2,1)S(1)} %copy-done.3, bf16[2,2,256,128]{3,2,1,0:T(8,128)(2,1)S(1)} %copy-done.4), custom_call_target="tpu_custom_call" | custom-call | tf_op jit(solution)/shard_map/inverse/pallas_call | solution.py:426
  (1 shorter events, 0.0 us)
Async XLA Ops:
  0.0 40.3 %copy-start.6 = (bf16[20,20]{1,0:T(8,128)(2,1)S(1)}, bf16[20,20]{1,0:T(8,128)(2,1)}, u32[]{:S(2)}) copy-start(bf16[20,20]{1,0:T(8,128)(2,1)} %param.11) | copy-start | bytes 2404
  7.1 22.4 %collective-permute-start = (f32[1472,128]{1,0:T(8,128)S(1)}, f32[1472,128]{1,0:T(8,128)S(1)}, u32[]{:S(2)}, u32[]{:S(2)}) collective-permute-start(f32[1472,128]{1,0:T(8,128)S(1)} %get-tuple-element.14), channel_id=1, source_target_pairs={{0,1},{1,0},{2,3},{3,2},{4,5},{5,4},{6,7},{7,6},{8,9},{9,8},{10,11... | collective-permute-start | bytes 2261000 | tf_op jit(solution)/shard_map/ppermute | solution.py:471
  30.5 48.5 %all-to-all-start = ((f32[64,23,1,128]{3,2,1,0:T(1,128)}), f32[64,23,1,128]{3,2,1,0:T(1,128)}, u32[]{:S(2)}, u32[]{:S(2)}) async-start(f32[64,23,1,128]{3,2,1,0:T(1,128)} %bitcast.2), calls=%async_computation | async-start | bytes 1507328 | tf_op jit(solution)/shard_map/all_to_all | solution.py:477
  44.3 1.8 %copy-start.2 = (bf16[1,20,6,96,128]{4,3,2,1,0:T(8,128)(2,1)S(1)}, bf16[1,20,6,96,128]{4,3,2,1,0:T(8,128)(2,1)}, u32[]{:S(2)}) copy-start(bf16[1,20,6,96,128]{4,3,2,1,0:T(8,128)(2,1)} %param.9) | copy-start | bytes 8847364
  44.3 1.8 %copy-start.5 = (f32[20]{0:T(128)S(1)}, f32[20]{0:T(128)}, u32[]{:S(2)}) copy-start(f32[20]{0:T(128)} %bias) | copy-start | bytes 244
  49.7 2.5 %copy-start = (f32[20,6,96,128]{3,2,1,0:T(8,128)}, f32[20,6,96,128]{3,2,1,0:T(8,128)S(1)}, u32[]{:S(2)}) copy-start(f32[20,6,96,128]{3,2,1,0:T(8,128)S(1)} %pointwise.1.base) | copy-start | bytes 17694724
  79.0 59.1 %copy-start.1 = (f32[20,6,96,128]{3,2,1,0:T(8,128)S(1)}, f32[20,6,96,128]{3,2,1,0:T(8,128)}, u32[]{:S(2)}) copy-start(f32[20,6,96,128]{3,2,1,0:T(8,128)} %copy-done) | copy-start | bytes 17694724
  79.0 59.1 %copy-start.3 = (bf16[2,384,256]{2,1,0:T(8,128)(2,1)S(1)}, bf16[2,384,256]{2,1,0:T(8,128)(2,1)}, u32[]{:S(2)}) copy-start(bf16[2,384,256]{2,1,0:T(8,128)(2,1)} %constant.20.clone.y_table) | copy-start | bytes 1179652
  79.0 59.1 %copy-start.4 = (bf16[2,2,256,128]{3,2,1,0:T(8,128)(2,1)S(1)}, bf16[2,2,256,128]{3,2,1,0:T(8,128)(2,1)}, u32[]{:S(2)}) copy-start(bf16[2,2,256,128]{3,2,1,0:T(8,128)(2,1)} %constant.21.clone.z_table) | copy-start | bytes 786436
  130.9 7.2 %collective-permute-start.1 = (f32[1472,128]{1,0:T(8,128)S(1)}, f32[1472,128]{1,0:T(8,128)S(1)}, u32[]{:S(2)}, u32[]{:S(2)}) collective-permute-start(f32[1472,128]{1,0:T(8,128)S(1)} %bitcast.11), channel_id=1, source_target_pairs={{0,1},{1,0},{2,3},{3,2},{4,5},{5,4},{6,7},{7,6},{8,9},{9,8},{10,11... | collective-permute-start | bytes 2261000 | tf_op jit(solution)/shard_map/ppermute | solution.py:471

commit v3 on v2

--- a/solution.py
+++ b/solution.py
@@ -65,8 +65,15 @@
 def z_forward_table(y_devices):
     tables = []
     for kz in z_order(y_devices):
-        angle = np.tile(angles(kz, np.arange(NZ), NZ).T, (1, QUAD))
-        tables.append(halves(np.concatenate([np.cos(angle), -np.sin(angle)], 1)))
+        angle = angles(kz, np.arange(NZ), NZ).T
+        parts = np.stack([np.cos(angle), -np.sin(angle)])
+        table = np.zeros((2, 2, NZ, 2, 2, MZ))
+        for c in range(2):
+            for s in range(2):
+                table[0, c, :, s, c] = parts[s]
+                table[1, c, :, s, c] = parts[1 - s]
+        table = halves(table.reshape(2, 2 * NZ, 4 * MZ))
+        tables.append(np.concatenate([table[0], table[1]], 2))
     return np.stack(tables)
 
 
@@ -116,15 +123,14 @@
     for kz in z_order(y_devices):
         angle = angles(kz, np.arange(NZ), NZ)
         weight = np.where(kz == 0, 1.0, 2.0)[:, None] / (NX * NY * NZ)
-        cosine = np.tile(np.cos(angle) * weight, (QUAD, 1))
-        sine = np.tile(np.sin(angle) * weight, (QUAD, 1))
-        tables.append(halves(np.concatenate([cosine, -sine], 0)))
+        parts = np.stack([np.cos(angle) * weight, -np.sin(angle) * weight])
+        table = np.zeros((2, 2, 2, MZ, 2, NZ))
+        for c in range(2):
+            for s in range(2):
+                table[0, s, c, :, c] = parts[s]
+                table[1, s, c, :, c] = parts[1 - s]
+        tables.append(np.swapaxes(halves(table.reshape(2, 4 * MZ, 2 * NZ)), 0, 1))
     return np.stack(tables)
-
-
-def own_block(table, c, dim):
-    at = lax.broadcasted_iota(jnp.int32, table.shape, dim) // MZ % QUAD
-    return jnp.where(at == c, table.astype(jnp.float32), 0.0).astype(jnp.bfloat16)
 
 
 def lane_of_part(shape):
@@ -151,7 +157,7 @@
 
 
 def forward_kernel(
-    x_local, place, field, z_tables, y_tables, own, other, cells, z_table, y_table, spread, z_hat, rows, loaded
+    x_local, place, field, z_tables, y_tables, own, other, cells, z_table, y_table, z_hat, rows, loaded
 ):
     channels, _, y_local, _ = field.shape
     groups = channels // QUAD
@@ -171,24 +177,33 @@
     tables[1].start()
     for x in order[X_FORWARD:]:
         loads[x].start()
-    tables[0].wait()
-    for part in range(2):
-        for c in range(QUAD):
-            spread[part, c * NZ : (c + 1) * NZ, :] = own_block(z_table[part], c, 1)
     last = {}
     for first in range(0, x_local, X_FORWARD):
         chunk = order[first : first + X_FORWARD]
         for x in chunk:
             loads[x].wait()
-        inputs = jnp.concatenate(
-            [
-                jnp.concatenate([cells[x, QUAD * g + c] for c in range(QUAD)], 1)
-                for x in chunk
-                for g in range(groups)
-            ],
-            0,
-        )
-        z_hat[first // X_FORWARD] = dot(inputs, spread[0]) + dot(inputs, spread[1])
+        if first == 0:
+            tables[0].wait()
+        for i, x in enumerate(chunk):
+            even, odd = (
+                dot(
+                    jnp.concatenate(
+                        [
+                            jnp.concatenate([cells[x, QUAD * g + 2 * k], cells[x, QUAD * g + 2 * k + 1]], 1)
+                            for g in range(groups)
+                        ],
+                        0,
+                    ),
+                    z_table[k],
+                )
+                for k in range(2)
+            )
+            even = even[:, :per_x] + even[:, per_x:]
+            odd = odd[:, :per_x] + odd[:, per_x:]
+            lower = lax.broadcasted_iota(jnp.int32, even.shape, 1) < per_x // 2
+            at = pl.ds(i * groups * y_local, groups * y_local)
+            z_hat[first // X_FORWARD, at, :per_x] = jnp.where(lower, even, odd)
+            z_hat[first // X_FORWARD, at, per_x:] = pltpu.roll(jnp.where(lower, odd, even), per_x // 2, 1)
         if first == 0:
             tables[1].wait()
         for i, x in enumerate(chunk):
@@ -234,7 +249,6 @@
                 pltpu.VMEM((x_local, channels, y_local, NZ), field.dtype),
                 pltpu.VMEM(z_table.shape[1:], jnp.bfloat16),
                 pltpu.VMEM(y_table.shape[1:], jnp.bfloat16),
-                pltpu.VMEM((2, QUAD * NZ, 2 * QUAD * MZ), jnp.bfloat16),
                 pltpu.VMEM((x_local // X_FORWARD, lines, 2 * QUAD * MZ), jnp.float32),
                 pltpu.VMEM((x_local, Y_BLOCKS, LANES + MP, LANES), jnp.float32),
                 pltpu.SemaphoreType.DMA((x_local + 2,)),
@@ -247,12 +261,15 @@
     )(place, in_hbm(field), in_hbm(jnp.asarray(z_table)), in_hbm(jnp.asarray(y_table)))
 
 
-def mix_kernel(x_local, payload, weights, table_hbm, result, table, spectrum, mixed, done):
+def mix_kernel(x_local, payload_hbm, weights, table_hbm, result, payload, table, spectrum, mixed, done, arrived):
     channels = weights.shape[1]
     sent = x_local * QUAD - 1
     x_devices = payload.shape[0] // sent
+    arrival = pltpu.make_async_copy(payload_hbm, payload, arrived)
+    arrival.start()
     load = pltpu.make_async_copy(table_hbm, table, done)
     load.start()
+    arrival.wait()
 
     def row_of(row):
         return pl.ds(row, x_devices, stride=sent)
@@ -310,17 +327,19 @@
     return pl.pallas_call(
         functools.partial(mix_kernel, x_local),
         out_shape=jax.ShapeDtypeStruct(payload.shape, jnp.float32),
-        in_specs=[vmem, vmem, pl.BlockSpec(memory_space=pltpu.HBM)],
+        in_specs=[pl.BlockSpec(memory_space=pltpu.HBM), vmem, pl.BlockSpec(memory_space=pltpu.HBM)],
         out_specs=vmem,
         scratch_shapes=[
+            pltpu.VMEM(payload.shape, jnp.float32),
             pltpu.VMEM(table.shape, jnp.bfloat16),
             pltpu.VMEM((QUAD, 2, HALF, LANES), jnp.float32),
             pltpu.VMEM((QUAD, LANES + MP, 2 * LANES), jnp.float32),
             pltpu.SemaphoreType.DMA,
+            pltpu.SemaphoreType.DMA,
         ],
         compiler_params=pltpu.CompilerParams(vmem_limit_bytes=20 * MIB),
         name="mix",
-    )(payload, weights, in_hbm(jnp.asarray(table)))
+    )(in_hbm(payload), weights, in_hbm(jnp.asarray(table)))
 
 
 def pointwise_kernel(field, local, bias, out):
@@ -356,16 +375,12 @@
     )(field, local, bias)
 
 
-def inverse_kernel(place, own, other, base, y_table, z_table, out, spread, rows, modes, lines, total, cells, stored):
+def inverse_kernel(place, own, other, base, y_table, z_table, out, rows, modes, lines, total, cells, stored):
     del place
     channels, x_local, y_local, _ = base.shape
     groups = channels // QUAD
     half = MZ // 2
     sent = x_local * QUAD - 1
-    for part in range(2):
-        for c in range(QUAD):
-            spread[part, :, c * NZ : (c + 1) * NZ] = own_block(z_table[0, part], c, 0)
-
     def row_of(block, row):
         return pl.ds(block * sent + row, half, stride=Y_BLOCKS * sent)
 
@@ -397,19 +412,24 @@
             parts = parts[: 2 * y_local] + parts[2 * y_local :]
             for i in range(X_INVERSE):
                 at = pl.ds(((first + i) * groups + g) * y_local, y_local)
-                for s in range(2):
-                    high, low = split(parts[s * y_local : (s + 1) * y_local, i * LANES : (i + 1) * LANES])
-                    lines[0, at, s * LANES : (s + 1) * LANES] = high
-                    lines[1, at, s * LANES : (s + 1) * LANES] = low
+                real = parts[:y_local, i * LANES : (i + 1) * LANES]
+                imag = pltpu.roll(parts[y_local:, i * LANES : (i + 1) * LANES], LANES // 2, 1)
+                lower = lax.broadcasted_iota(jnp.int32, real.shape, 1) < LANES // 2
+                for k, value in enumerate((jnp.where(lower, real, imag), jnp.where(lower, imag, real))):
+                    high, low = split(value)
+                    lines[k, at, :LANES] = high
+                    lines[k, at, LANES:] = low
         at = pl.ds(first * groups * y_local, X_INVERSE * groups * y_local)
-        high, low = lines[0, at, :], lines[1, at, :]
-        total[at, :] = dot(high, spread[0]) + dot(low, spread[0]) + dot(high, spread[1])
+        for k in range(2):
+            high, low = z_table[0, k, 0], z_table[0, k, 1]
+            both = dot(lines[k, at, :], jnp.concatenate([high, high], 0))
+            total[k, at, :] = both + dot(lines[k, at, :LANES], low)
         scale = math.sqrt(2 / math.pi)
         for x in chunk:
             for o in range(channels):
                 g, c = o // QUAD, o % QUAD
                 at = pl.ds((x * groups + g) * y_local, y_local)
-                value = total[at, c * NZ : (c + 1) * NZ] + base[o, x]
+                value = total[c // 2, at, c % 2 * NZ : (c % 2 + 1) * NZ] + base[o, x]
                 inner = value * (scale + (scale * 0.044715) * (value * value))
                 scaled = 0.5 * value
                 cells[x, o] = (scaled + scaled * jnp.tanh(inner)).astype(out.dtype)
@@ -434,15 +454,14 @@
                 vmem,
                 vmem,
                 pl.BlockSpec((1, *y_table.shape[1:]), lambda x, p: (p[0], 0, 0)),
-                pl.BlockSpec((1, *z_table.shape[1:]), lambda x, p: (p[0], 0, 0, 0)),
+                pl.BlockSpec((1, *z_table.shape[1:]), lambda x, p: (p[0], 0, 0, 0, 0)),
             ],
             out_specs=pl.BlockSpec(memory_space=pltpu.HBM),
             scratch_shapes=[
-                pltpu.VMEM((2, 2 * QUAD * MZ, QUAD * NZ), jnp.bfloat16),
                 pltpu.VMEM((x_local, Y_BLOCKS, LANES, LANES), jnp.float32),
                 pltpu.VMEM((x_local, Y_BLOCKS, LANES, LANES), jnp.float32),
                 pltpu.VMEM((2, lines, 2 * LANES), jnp.bfloat16),
-                pltpu.VMEM((lines, QUAD * NZ), jnp.float32),
+                pltpu.VMEM((2, lines, 2 * NZ), jnp.float32),
                 pltpu.VMEM((x_local, channels, y_local, NZ), dtype),
                 pltpu.SemaphoreType.DMA((x_local,)),
             ],

time: 144 us -> 141 us (0.979)
  Pallas kernels: 22 us -> 17.5 us
    pallas_call x1, Pallas kernels: 7.13 us -> 4.26 us  [forward(): pl.pallas_call(functools.partial(forward_kernel, x_local), out_shape=(pay...]
  transfers between devices with their start and end apart: 3 -> 3, of which waited for: 3 -> 3; matrix products, arithmetic and copies ran while one was open for 3% -> 4% of each run, Pallas kernels for 2% -> 3%
where the time goes in v3:
time: 141 us; the launch traced here: 140 us
  blocking collectives  46.1 us (33%)
  starting transfers between devices  35.7 us (25%)
  waiting for transfers between devices  30.4 us (22%)
  Pallas kernels  17.5 us (12%)
  local copies, waits for them, and re-layouts  9.12 us (6%)
    all_to_all x1, blocking collectives, exchanged(): return lax.all_to_all(blocks, axis, 0, 0, tiled=True).reshape(rows.shape)  46.1 us
    all_to_all x1, waiting for transfers between devices, exchanged(): return lax.all_to_all(blocks, axis, 0, 0, tiled=True).reshape(rows.shape)  26.7 us
    ppermute x2, starting transfers between devices, swapped(): lax.ppermute(x, axis, [(d, (d + 1) % devices) for d in range(devices)])  25.9 us
    all_to_all x1, starting transfers between devices, exchanged(): return lax.all_to_all(blocks, axis, 0, 0, tiled=True).reshape(rows.shape)  9.8 us
    pallas_call x1, Pallas kernels, inverse(): pl.pallas_call(inverse_kernel, out_shape=jax.ShapeDtypeStruct(base.shape,...  5.18 us
    pallas_call x1, Pallas kernels, mix(): pl.pallas_call(functools.partial(mix_kernel, x_local), out_shape=jax.Shap...  4.45 us
    unnamed x14, local copies, waits for them, and re-layouts  4.36 us
    pallas_call x1, Pallas kernels, forward(): pl.pallas_call(functools.partial(forward_kernel, x_local), out_shape=(pay...  4.26 us
  transfers between devices with their start and end apart: 3, of which 3 were waited for; matrix products, arithmetic and copies ran while one was open for 4% of the time, Pallas kernels for 3%

profile of v3, /device:TPU:33, one launch (start us, length us, event | category | flops | bytes accessed | tf_op | source)
XLA Modules:
  0.0 140.2 jit_solution(2146130101515882560)
XLA Ops:
  0.0 0.0 copy-start.6
  0.0 4.3 %forward.1 = (f32[1472,128]{1,0:T(8,128)S(1)}, f32[1472,128]{1,0:T(8,128)S(1)}) custom-call(s32[1]{0:T(128)} %bitcast.place, bf16[20,6,96,128]{3,2,1,0:T(8,128)(2,1)} %bitcast.8, bf16[2,2,256,256]{3,2,1,0:T(8,128)(2,1)} %constant.17.clone.z_tables, bf16[2,256,192]{2,1,0:T(8,128)(2,1)} %constant.18.clone.y_tables), custom_call_target="tpu_custom_call" | custom-call | tf_op jit(solution)/shard_map/forward/pallas_call | solution.py:240
  4.3 20.5 %collective-permute-start = (f32[1472,128]{1,0:T(8,128)S(1)}, f32[1472,128]{1,0:T(8,128)S(1)}, u32[]{:S(2)}, u32[]{:S(2)}) collective-permute-start(f32[1472,128]{1,0:T(8,128)S(1)} %get-tuple-element.14), channel_id=1, source_target_pairs={{0,1},{1,0},{2,3},{3,2},{4,5},{5,4},{6,7},{7,6},{8,9},{9,8},{10,11... | collective-permute-start | bytes 2261000 | tf_op jit(solution)/shard_map/ppermute | solution.py:490
  24.8 1.9 %collective-permute-done = f32[1472,128]{1,0:T(8,128)S(1)} collective-permute-done((f32[1472,128]{1,0:T(8,128)S(1)}, f32[1472,128]{1,0:T(8,128)S(1)}, u32[]{:S(2)}, u32[]{:S(2)}) %collective-permute-start) | collective-permute-done | bytes 753696 | tf_op jit(solution)/shard_map/ppermute | solution.py:490
  26.7 0.9 add.5
  27.6 9.8 %all-to-all-start = ((f32[64,23,1,128]{3,2,1,0:T(1,128)}), f32[64,23,1,128]{3,2,1,0:T(1,128)}, u32[]{:S(2)}, u32[]{:S(2)}) async-start(f32[64,23,1,128]{3,2,1,0:T(1,128)} %bitcast.2), calls=%async_computation | async-start | bytes 1507328 | tf_op jit(solution)/shard_map/all_to_all | solution.py:496
  37.4 0.0 copy-done.6
  37.5 0.1 copy.15
  37.6 0.2 broadcast_multiply_fusion
  37.8 1.2 mul.20.local
  39.0 2.5 %copy.16 = bf16[2,20,20,12,96]{4,3,2,1,0:T(8,128)(2,1)S(1)} copy(bf16[2,20,20,12,96]{4,0,3,2,1:T(2,128)(2,1)} %param.10) | data formatting | bytes 3686400 | tf_op jit(solution)/shard_map/optimization_barrier | solution.py:505
  41.4 0.0 copy-start.2
  41.4 0.0 copy-start.5
  41.5 1.0 pad.4.weights
  42.5 0.8 copy-done.2
  43.3 0.0 copy-done.5
  43.3 3.6 %pointwise.1.base = f32[20,6,96,128]{3,2,1,0:T(8,128)S(1)} custom-call(bf16[20,6,96,128]{3,2,1,0:T(8,128)(2,1)S(1)} %bitcast.9, bf16[320,320]{1,0:T(8,128)(2,1)S(1)} %mul.20.local, f32[20]{0:T(128)S(1)} %copy-done.5), custom_call_target="tpu_custom_call" | custom-call | flops 943718400 | bytes 8847360 | tf_op jit(solution)/shard_map/pointwise/pallas_call | solution.py:362
  46.9 0.0 copy-start
  46.9 2.5 %copy-done = f32[20,6,96,128]{3,2,1,0:T(8,128)} copy-done((f32[20,6,96,128]{3,2,1,0:T(8,128)}, f32[20,6,96,128]{3,2,1,0:T(8,128)S(1)}, u32[]{:S(2)}) %copy-start) | copy-done | bytes 5898264
  49.4 26.7 %all-to-all-done = f32[64,23,1,128]{3,2,1,0:T(1,128)} async-done(((f32[64,23,1,128]{3,2,1,0:T(1,128)}), f32[64,23,1,128]{3,2,1,0:T(1,128)}, u32[]{:S(2)}, u32[]{:S(2)}) %all-to-all-start) | async-done | bytes 753696 | tf_op jit(solution)/shard_map/all_to_all | solution.py:496
  76.1 0.0 copy-start.1
  76.1 0.0 copy-start.3
  76.1 4.5 %mix.1 = f32[1472,128]{1,0:T(8,128)S(1)} custom-call(f32[1472,128]{1,0:T(8,128)} %bitcast.3.payload_hbm, bf16[2,20,20,16,128]{4,3,2,1,0:T(8,128)(2,1)S(1)} %pad.4.weights, bf16[2,384,256]{2,1,0:T(8,128)(2,1)} %constant.19.clone.table_hbm), custom_call_target="tpu_custom_call" | custom-call | tf_op jit(solution)/shard_map/mix/pallas_call | solution.py:327
  80.6 46.1 %all_to_all.10 = f32[64,23,1,128]{3,2,1,0:T(1,128)S(1)} all-to-all(f32[64,23,1,128]{3,2,1,0:T(1,128)S(1)} %bitcast.12), channel_id=1, replica_groups=mesh['groups'=2,'px'=64,'py'=2] {'px'}, dimensions={0} | all-to-all | bytes 1507328 | tf_op jit(solution)/shard_map/all_to_all | solution.py:496
  126.7 5.4 %collective-permute-start.1 = (f32[1472,128]{1,0:T(8,128)S(1)}, f32[1472,128]{1,0:T(8,128)S(1)}, u32[]{:S(2)}, u32[]{:S(2)}) collective-permute-start(f32[1472,128]{1,0:T(8,128)S(1)} %bitcast.10), channel_id=1, source_target_pairs={{0,1},{1,0},{2,3},{3,2},{4,5},{5,4},{6,7},{7,6},{8,9},{9,8},{10,11... | collective-permute-start | bytes 2261000 | tf_op jit(solution)/shard_map/ppermute | solution.py:490
  132.0 1.9 %collective-permute-done.1.other = f32[1472,128]{1,0:T(8,128)S(1)} collective-permute-done((f32[1472,128]{1,0:T(8,128)S(1)}, f32[1472,128]{1,0:T(8,128)S(1)}, u32[]{:S(2)}, u32[]{:S(2)}) %collective-permute-start.1) | collective-permute-done | bytes 753696 | tf_op jit(solution)/shard_map/ppermute | solution.py:490
  133.9 0.0 copy-done.1
  133.9 0.0 copy-done.3
  133.9 0.0 copy-start.4
  133.9 1.0 copy-done.4
  134.9 5.2 %inverse.1 = bf16[20,6,96,128]{3,2,1,0:T(8,128)(2,1)} custom-call(s32[1]{0:T(128)} %bitcast.place, f32[1472,128]{1,0:T(8,128)S(1)} %bitcast.11, f32[1472,128]{1,0:T(8,128)S(1)} %collective-permute-done.1.other, f32[20,6,96,128]{3,2,1,0:T(8,128)S(1)} %copy-done.1, bf16[2,384,256]{2,1,0:T(8,128)(2,1)S(1)} %copy-done.4, bf16[2,2,2,128,256]{4,3,2,1,0:T(8,128)(2,1)S(1)} %copy-done.3), custom_call_target="tpu_custom_call" | custom-call | tf_op jit(solution)/shard_map/inverse/pallas_call | solution.py:446
  (1 shorter events, 0.0 us)
Async XLA Ops:
  0.0 37.4 %copy-start.6 = (bf16[20,20]{1,0:T(8,128)(2,1)S(1)}, bf16[20,20]{1,0:T(8,128)(2,1)}, u32[]{:S(2)}) copy-start(bf16[20,20]{1,0:T(8,128)(2,1)} %param.11) | copy-start | bytes 2404
  4.3 22.4 %collective-permute-start = (f32[1472,128]{1,0:T(8,128)S(1)}, f32[1472,128]{1,0:T(8,128)S(1)}, u32[]{:S(2)}, u32[]{:S(2)}) collective-permute-start(f32[1472,128]{1,0:T(8,128)S(1)} %get-tuple-element.14), channel_id=1, source_target_pairs={{0,1},{1,0},{2,3},{3,2},{4,5},{5,4},{6,7},{7,6},{8,9},{9,8},{10,11... | collective-permute-start | bytes 2261000 | tf_op jit(solution)/shard_map/ppermute | solution.py:490
  27.6 48.5 %all-to-all-start = ((f32[64,23,1,128]{3,2,1,0:T(1,128)}), f32[64,23,1,128]{3,2,1,0:T(1,128)}, u32[]{:S(2)}, u32[]{:S(2)}) async-start(f32[64,23,1,128]{3,2,1,0:T(1,128)} %bitcast.2), calls=%async_computation | async-start | bytes 1507328 | tf_op jit(solution)/shard_map/all_to_all | solution.py:496
  41.4 1.8 %copy-start.2 = (bf16[1,20,6,96,128]{4,3,2,1,0:T(8,128)(2,1)S(1)}, bf16[1,20,6,96,128]{4,3,2,1,0:T(8,128)(2,1)}, u32[]{:S(2)}) copy-start(bf16[1,20,6,96,128]{4,3,2,1,0:T(8,128)(2,1)} %param.9) | copy-start | bytes 8847364
  41.4 1.8 %copy-start.5 = (f32[20]{0:T(128)S(1)}, f32[20]{0:T(128)}, u32[]{:S(2)}) copy-start(f32[20]{0:T(128)} %bias) | copy-start | bytes 244
  46.9 2.5 %copy-start = (f32[20,6,96,128]{3,2,1,0:T(8,128)}, f32[20,6,96,128]{3,2,1,0:T(8,128)S(1)}, u32[]{:S(2)}) copy-start(f32[20,6,96,128]{3,2,1,0:T(8,128)S(1)} %pointwise.1.base) | copy-start | bytes 17694724
  76.1 57.7 %copy-start.1 = (f32[20,6,96,128]{3,2,1,0:T(8,128)S(1)}, f32[20,6,96,128]{3,2,1,0:T(8,128)}, u32[]{:S(2)}) copy-start(f32[20,6,96,128]{3,2,1,0:T(8,128)} %copy-done) | copy-start | bytes 17694724
  76.1 57.7 %copy-start.3 = (bf16[2,2,2,128,256]{4,3,2,1,0:T(8,128)(2,1)S(1)}, bf16[2,2,2,128,256]{4,3,2,1,0:T(8,128)(2,1)}, u32[]{:S(2)}) copy-start(bf16[2,2,2,128,256]{4,3,2,1,0:T(8,128)(2,1)} %constant.21.clone.z_table) | copy-start | bytes 1572868
  126.7 7.2 %collective-permute-start.1 = (f32[1472,128]{1,0:T(8,128)S(1)}, f32[1472,128]{1,0:T(8,128)S(1)}, u32[]{:S(2)}, u32[]{:S(2)}) collective-permute-start(f32[1472,128]{1,0:T(8,128)S(1)} %bitcast.10), channel_id=1, source_target_pairs={{0,1},{1,0},{2,3},{3,2},{4,5},{5,4},{6,7},{7,6},{8,9},{9,8},{10,11... | collective-permute-start | bytes 2261000 | tf_op jit(solution)/shard_map/ppermute | solution.py:490
  133.9 1.0 copy-start.4

commit v4 on v3

--- a/solution.py
+++ b/solution.py
@@ -375,8 +375,11 @@
     )(field, local, bias)
 
 
-def inverse_kernel(place, own, other, base, y_table, z_table, out, rows, modes, lines, total, cells, stored):
-    del place
+def inverse_kernel(
+    place, own, other, base, y_table, z_tables, out, z_table, rows, modes, lines, total, cells, stored, loaded
+):
+    load = pltpu.make_async_copy(z_tables.at[place[0]], z_table, loaded)
+    load.start()
     channels, x_local, y_local, _ = base.shape
     groups = channels // QUAD
     half = MZ // 2
@@ -420,8 +423,10 @@
                     lines[k, at, :LANES] = high
                     lines[k, at, LANES:] = low
         at = pl.ds(first * groups * y_local, X_INVERSE * groups * y_local)
+        if first == 0:
+            load.wait()
         for k in range(2):
-            high, low = z_table[0, k, 0], z_table[0, k, 1]
+            high, low = z_table[k, 0], z_table[k, 1]
             both = dot(lines[k, at, :], jnp.concatenate([high, high], 0))
             total[k, at, :] = both + dot(lines[k, at, :LANES], low)
         scale = math.sqrt(2 / math.pi)
@@ -454,23 +459,25 @@
                 vmem,
                 vmem,
                 pl.BlockSpec((1, *y_table.shape[1:]), lambda x, p: (p[0], 0, 0)),
-                pl.BlockSpec((1, *z_table.shape[1:]), lambda x, p: (p[0], 0, 0, 0, 0)),
+                pl.BlockSpec(memory_space=pltpu.HBM),
             ],
             out_specs=pl.BlockSpec(memory_space=pltpu.HBM),
             scratch_shapes=[
+                pltpu.VMEM(z_table.shape[1:], jnp.bfloat16),
                 pltpu.VMEM((x_local, Y_BLOCKS, LANES, LANES), jnp.float32),
                 pltpu.VMEM((x_local, Y_BLOCKS, LANES, LANES), jnp.float32),
                 pltpu.VMEM((2, lines, 2 * LANES), jnp.bfloat16),
                 pltpu.VMEM((2, lines, 2 * NZ), jnp.float32),
                 pltpu.VMEM((x_local, channels, y_local, NZ), dtype),
                 pltpu.SemaphoreType.DMA((x_local,)),
+                pltpu.SemaphoreType.DMA,
             ],
         ),
         compiler_params=pltpu.CompilerParams(
             dimension_semantics=("arbitrary",), vmem_limit_bytes=36 * MIB
         ),
         name="inverse",
-    )(place, own, other, base, jnp.asarray(y_table), jnp.asarray(z_table))
+    )(place, own, other, base, jnp.asarray(y_table), in_hbm(jnp.asarray(z_table)))
 
 
 def spread_weights(spectral_weight):

time: 141 us -> 140 us (level)
    unnamed x14 -> x12, local copies, waits for them, and re-layouts: 4.36 us -> 3.35 us
where the time goes in v4:
time: 140 us
  blocking collectives  46.1 us (33%)
  starting transfers between devices  35.7 us (26%)
  waiting for transfers between devices  30.5 us (22%)
  Pallas kernels  17.8 us (13%)
  local copies, waits for them, and re-layouts  8.11 us (6%)
    all_to_all x1, blocking collectives, exchanged(): return lax.all_to_all(blocks, axis, 0, 0, tiled=True).reshape(rows.shape)  46.1 us
    all_to_all x1, waiting for transfers between devices, exchanged(): return lax.all_to_all(blocks, axis, 0, 0, tiled=True).reshape(rows.shape)  26.7 us
    ppermute x2, starting transfers between devices, swapped(): lax.ppermute(x, axis, [(d, (d + 1) % devices) for d in range(devices)])  25.9 us
    all_to_all x1, starting transfers between devices, exchanged(): return lax.all_to_all(blocks, axis, 0, 0, tiled=True).reshape(rows.shape)  9.8 us
    pallas_call x1, Pallas kernels, inverse(): pl.pallas_call(inverse_kernel, out_shape=jax.ShapeDtypeStruct(base.shape,...  5.52 us
    pallas_call x1, Pallas kernels, mix(): pl.pallas_call(functools.partial(mix_kernel, x_local), out_shape=jax.Shap...  4.45 us
    pallas_call x1, Pallas kernels, forward(): pl.pallas_call(functools.partial(forward_kernel, x_local), out_shape=(pay...  4.26 us
    ppermute x2, waiting for transfers between devices, swapped(): lax.ppermute(x, axis, [(d, (d + 1) % devices) for d in range(devices)])  3.73 us
  transfers between devices with their start and end apart: 3, of which 3 were waited for; matrix products, arithmetic and copies ran while one was open for 4% of the time, Pallas kernels for 3%

profile of v4, /device:TPU:33, one launch (start us, length us, event | category | flops | bytes accessed | tf_op | source)
XLA Modules:
  0.0 139.6 jit_solution(9735274723873619674)
XLA Ops:
  0.0 0.0 copy-start.5
  0.0 4.3 %forward.1 = (f32[1472,128]{1,0:T(8,128)S(1)}, f32[1472,128]{1,0:T(8,128)S(1)}) custom-call(s32[1]{0:T(128)} %bitcast.place, bf16[20,6,96,128]{3,2,1,0:T(8,128)(2,1)} %bitcast.8, bf16[2,2,256,256]{3,2,1,0:T(8,128)(2,1)} %constant.17.clone.z_tables, bf16[2,256,192]{2,1,0:T(8,128)(2,1)} %constant.18.clone.y_tables), custom_call_target="tpu_custom_call" | custom-call | tf_op jit(solution)/shard_map/forward/pallas_call | solution.py:240
  4.3 20.5 %collective-permute-start = (f32[1472,128]{1,0:T(8,128)S(1)}, f32[1472,128]{1,0:T(8,128)S(1)}, u32[]{:S(2)}, u32[]{:S(2)}) collective-permute-start(f32[1472,128]{1,0:T(8,128)S(1)} %get-tuple-element.14), channel_id=1, source_target_pairs={{0,1},{1,0},{2,3},{3,2},{4,5},{5,4},{6,7},{7,6},{8,9},{9,8},{10,11... | collective-permute-start | bytes 2261000 | tf_op jit(solution)/shard_map/ppermute | solution.py:497
  24.8 1.9 %collective-permute-done = f32[1472,128]{1,0:T(8,128)S(1)} collective-permute-done((f32[1472,128]{1,0:T(8,128)S(1)}, f32[1472,128]{1,0:T(8,128)S(1)}, u32[]{:S(2)}, u32[]{:S(2)}) %collective-permute-start) | collective-permute-done | bytes 753696 | tf_op jit(solution)/shard_map/ppermute | solution.py:497
  26.7 0.9 add.5
  27.6 9.8 %all-to-all-start = ((f32[64,23,1,128]{3,2,1,0:T(1,128)}), f32[64,23,1,128]{3,2,1,0:T(1,128)}, u32[]{:S(2)}, u32[]{:S(2)}) async-start(f32[64,23,1,128]{3,2,1,0:T(1,128)} %bitcast.2), calls=%async_computation | async-start | bytes 1507328 | tf_op jit(solution)/shard_map/all_to_all | solution.py:503
  37.4 0.0 copy-done.5
  37.5 0.1 copy.15
  37.6 0.2 broadcast_multiply_fusion
  37.8 1.2 mul.20.local
  39.0 2.5 %copy.16 = bf16[2,20,20,12,96]{4,3,2,1,0:T(8,128)(2,1)S(1)} copy(bf16[2,20,20,12,96]{4,0,3,2,1:T(2,128)(2,1)} %param.10) | data formatting | bytes 3686400 | tf_op jit(solution)/shard_map/optimization_barrier | solution.py:512
  41.4 0.0 copy-start.2
  41.4 0.0 copy-start.4
  41.5 1.0 pad.4.weights
  42.5 0.8 copy-done.2
  43.3 0.0 copy-done.4
  43.3 3.6 %pointwise.1.base = f32[20,6,96,128]{3,2,1,0:T(8,128)S(1)} custom-call(bf16[20,6,96,128]{3,2,1,0:T(8,128)(2,1)S(1)} %bitcast.9, bf16[320,320]{1,0:T(8,128)(2,1)S(1)} %mul.20.local, f32[20]{0:T(128)S(1)} %copy-done.4), custom_call_target="tpu_custom_call" | custom-call | flops 943718400 | bytes 8847360 | tf_op jit(solution)/shard_map/pointwise/pallas_call | solution.py:362
  46.9 0.0 copy-start
  46.9 2.5 %copy-done = f32[20,6,96,128]{3,2,1,0:T(8,128)} copy-done((f32[20,6,96,128]{3,2,1,0:T(8,128)}, f32[20,6,96,128]{3,2,1,0:T(8,128)S(1)}, u32[]{:S(2)}) %copy-start) | copy-done | bytes 5898264
  49.4 26.7 %all-to-all-done = f32[64,23,1,128]{3,2,1,0:T(1,128)} async-done(((f32[64,23,1,128]{3,2,1,0:T(1,128)}), f32[64,23,1,128]{3,2,1,0:T(1,128)}, u32[]{:S(2)}, u32[]{:S(2)}) %all-to-all-start) | async-done | bytes 753696 | tf_op jit(solution)/shard_map/all_to_all | solution.py:503
  76.1 0.0 copy-start.1
  76.1 0.0 copy-start.3
  76.1 4.5 %mix.1 = f32[1472,128]{1,0:T(8,128)S(1)} custom-call(f32[1472,128]{1,0:T(8,128)} %bitcast.3.payload_hbm, bf16[2,20,20,16,128]{4,3,2,1,0:T(8,128)(2,1)S(1)} %pad.4.weights, bf16[2,384,256]{2,1,0:T(8,128)(2,1)} %constant.19.clone.table_hbm), custom_call_target="tpu_custom_call" | custom-call | tf_op jit(solution)/shard_map/mix/pallas_call | solution.py:327
  80.6 46.1 %all_to_all.10 = f32[64,23,1,128]{3,2,1,0:T(1,128)S(1)} all-to-all(f32[64,23,1,128]{3,2,1,0:T(1,128)S(1)} %bitcast.12), channel_id=1, replica_groups=mesh['groups'=2,'px'=64,'py'=2] {'px'}, dimensions={0} | all-to-all | bytes 1507328 | tf_op jit(solution)/shard_map/all_to_all | solution.py:503
  126.7 5.4 %collective-permute-start.1 = (f32[1472,128]{1,0:T(8,128)S(1)}, f32[1472,128]{1,0:T(8,128)S(1)}, u32[]{:S(2)}, u32[]{:S(2)}) collective-permute-start(f32[1472,128]{1,0:T(8,128)S(1)} %bitcast.10), channel_id=1, source_target_pairs={{0,1},{1,0},{2,3},{3,2},{4,5},{5,4},{6,7},{7,6},{8,9},{9,8},{10,11... | collective-permute-start | bytes 2261000 | tf_op jit(solution)/shard_map/ppermute | solution.py:497
  132.0 1.9 %collective-permute-done.1.other = f32[1472,128]{1,0:T(8,128)S(1)} collective-permute-done((f32[1472,128]{1,0:T(8,128)S(1)}, f32[1472,128]{1,0:T(8,128)S(1)}, u32[]{:S(2)}, u32[]{:S(2)}) %collective-permute-start.1) | collective-permute-done | bytes 753696 | tf_op jit(solution)/shard_map/ppermute | solution.py:497
  133.9 0.0 copy-done.1
  133.9 0.0 copy-done.3
  133.9 5.5 %inverse.1 = bf16[20,6,96,128]{3,2,1,0:T(8,128)(2,1)} custom-call(s32[1]{0:T(128)} %bitcast.place, f32[1472,128]{1,0:T(8,128)S(1)} %bitcast.11, f32[1472,128]{1,0:T(8,128)S(1)} %collective-permute-done.1.other, f32[20,6,96,128]{3,2,1,0:T(8,128)S(1)} %copy-done.1, bf16[2,384,256]{2,1,0:T(8,128)(2,1)S(1)} %copy-done.3, ...), custom_call_target="tpu_custom_call" | custom-call | tf_op jit(solution)/shard_map/inverse/pallas_call | solution.py:451
  (1 shorter events, 0.0 us)
Async XLA Ops:
  0.0 37.4 %copy-start.5 = (bf16[20,20]{1,0:T(8,128)(2,1)S(1)}, bf16[20,20]{1,0:T(8,128)(2,1)}, u32[]{:S(2)}) copy-start(bf16[20,20]{1,0:T(8,128)(2,1)} %param.11) | copy-start | bytes 2404
  4.3 22.4 %collective-permute-start = (f32[1472,128]{1,0:T(8,128)S(1)}, f32[1472,128]{1,0:T(8,128)S(1)}, u32[]{:S(2)}, u32[]{:S(2)}) collective-permute-start(f32[1472,128]{1,0:T(8,128)S(1)} %get-tuple-element.14), channel_id=1, source_target_pairs={{0,1},{1,0},{2,3},{3,2},{4,5},{5,4},{6,7},{7,6},{8,9},{9,8},{10,11... | collective-permute-start | bytes 2261000 | tf_op jit(solution)/shard_map/ppermute | solution.py:497
  27.6 48.5 %all-to-all-start = ((f32[64,23,1,128]{3,2,1,0:T(1,128)}), f32[64,23,1,128]{3,2,1,0:T(1,128)}, u32[]{:S(2)}, u32[]{:S(2)}) async-start(f32[64,23,1,128]{3,2,1,0:T(1,128)} %bitcast.2), calls=%async_computation | async-start | bytes 1507328 | tf_op jit(solution)/shard_map/all_to_all | solution.py:503
  41.4 1.8 %copy-start.2 = (bf16[1,20,6,96,128]{4,3,2,1,0:T(8,128)(2,1)S(1)}, bf16[1,20,6,96,128]{4,3,2,1,0:T(8,128)(2,1)}, u32[]{:S(2)}) copy-start(bf16[1,20,6,96,128]{4,3,2,1,0:T(8,128)(2,1)} %param.9) | copy-start | bytes 8847364
  41.4 1.8 %copy-start.4 = (f32[20]{0:T(128)S(1)}, f32[20]{0:T(128)}, u32[]{:S(2)}) copy-start(f32[20]{0:T(128)} %bias) | copy-start | bytes 244
  46.9 2.5 %copy-start = (f32[20,6,96,128]{3,2,1,0:T(8,128)}, f32[20,6,96,128]{3,2,1,0:T(8,128)S(1)}, u32[]{:S(2)}) copy-start(f32[20,6,96,128]{3,2,1,0:T(8,128)S(1)} %pointwise.1.base) | copy-start | bytes 17694724
  76.1 57.7 %copy-start.1 = (f32[20,6,96,128]{3,2,1,0:T(8,128)S(1)}, f32[20,6,96,128]{3,2,1,0:T(8,128)}, u32[]{:S(2)}) copy-start(f32[20,6,96,128]{3,2,1,0:T(8,128)} %copy-done) | copy-start | bytes 17694724
  76.1 57.7 %copy-start.3 = (bf16[2,384,256]{2,1,0:T(8,128)(2,1)S(1)}, bf16[2,384,256]{2,1,0:T(8,128)(2,1)}, u32[]{:S(2)}) copy-start(bf16[2,384,256]{2,1,0:T(8,128)(2,1)} %constant.20.clone.y_table) | copy-start | bytes 1179652
  126.7 7.2 %collective-permute-start.1 = (f32[1472,128]{1,0:T(8,128)S(1)}, f32[1472,128]{1,0:T(8,128)S(1)}, u32[]{:S(2)}, u32[]{:S(2)}) collective-permute-start(f32[1472,128]{1,0:T(8,128)S(1)} %bitcast.10), channel_id=1, source_target_pairs={{0,1},{1,0},{2,3},{3,2},{4,5},{5,4},{6,7},{7,6},{8,9},{9,8},{10,11... | collective-permute-start | bytes 2261000 | tf_op jit(solution)/shard_map/ppermute | solution.py:497
